TPU v7x, 32 devices: a whole 2x2x4 slice. The times are simulated.
32 devices in a mesh: data: 2 (over x), tp: 4 (over z), sp: 4 (over y, core).
Axes of the slice: x: 2, y: 2, z: 4, core: 2. Of those that a mesh axis runs over, the one named last changes fastest.
Arguments:
- x: bfloat16 [2, 16, 256, 5120], P('data', 'sp', 'tp'), parts along dimension 0
- ln_gain: float32 [2, 2, 5120], replicated
- ln_bias: float32 [2, 2, 5120], replicated
- w_qkv: bfloat16 [2, 5120, 3, 40, 128], P(None, None, None, 'tp')
- w_out: bfloat16 [2, 40, 128, 5120], P(None, 'tp')
- w_up: bfloat16 [2, 5120, 13824], P(None, None, 'tp')
- w_down: bfloat16 [2, 13824, 5120], P(None, 'tp')
Outputs:
- output: bfloat16 [2, 16, 256, 5120], P('data', 'sp', 'tp'), parts along dimension 0
There are 2 independent parts. A program takes and returns all parts, laid end to end along the dimension named above; an argument that names none is the same for every part.
All inputs are finite; a program needn't handle non-finite values.
Results may differ from a plain program's by a relative error of at most 0.0172211.
Values are sent between devices in bfloat16 or wider.
A program may use at most 1 GiB of HBM per device.

v0:
```python
import jax
import jax.numpy as jnp
from jax import lax
from jax.sharding import PartitionSpec as P

SPATIAL_FORMS = ("btqhk,btshk->bthqs", "bthqs,btshk->btqhk")
TEMPORAL_FORMS = ("bqshk,btshk->bshqt", "bshqt,btshk->bqshk")


def layer_norm(residual, gain, shift):
    centered = residual.astype(jnp.float32)
    centered = centered - jnp.mean(centered, axis=-1, keepdims=True)
    variance = jnp.mean(centered * centered, axis=-1, keepdims=True)
    return (centered * lax.rsqrt(variance + 1e-6) * gain + shift).astype(jnp.bfloat16)


def local_block(residual, gain, shift, w_qkv, w_out, w_up, w_down, forms):
    head_size = w_qkv.shape[-1]
    gathered = lax.all_gather(layer_norm(residual, gain[0], shift[0]), "tp", axis=2, tiled=True)
    qkv_proj = jnp.einsum("btsd,dchk->cbtshk", gathered, w_qkv, preferred_element_type=jnp.float32).astype(jnp.bfloat16)
    scores = jnp.einsum(forms[0], qkv_proj[0], qkv_proj[1], preferred_element_type=jnp.float32) * head_size ** -0.5
    attn_prob = jax.nn.softmax(scores, axis=-1).astype(jnp.bfloat16)
    mixed = jnp.einsum(forms[1], attn_prob, qkv_proj[2], preferred_element_type=jnp.float32).astype(jnp.bfloat16)
    part_sum = jnp.einsum("btshk,hkd->btsd", mixed, w_out, preferred_element_type=jnp.float32)
    attn_out = lax.psum_scatter(part_sum, "tp", scatter_dimension=2, tiled=True).astype(jnp.bfloat16)
    hidden = (residual.astype(jnp.float32) + attn_out.astype(jnp.float32)).astype(jnp.bfloat16)
    gathered_mlp = lax.all_gather(layer_norm(hidden, gain[1], shift[1]), "tp", axis=2, tiled=True)
    up_proj = jnp.einsum("btsd,df->btsf", gathered_mlp, w_up, preferred_element_type=jnp.float32).astype(jnp.bfloat16)
    gelu_out = jax.nn.gelu(up_proj.astype(jnp.float32), approximate=True).astype(jnp.bfloat16)
    part_down = jnp.einsum("btsf,fd->btsd", gelu_out, w_down, preferred_element_type=jnp.float32)
    mlp_out = lax.psum_scatter(part_down, "tp", scatter_dimension=2, tiled=True).astype(jnp.bfloat16)
    return (hidden.astype(jnp.float32) + mlp_out.astype(jnp.float32)).astype(jnp.bfloat16)


def solution(mesh):
    act_spec = P("data", "sp", "tp", None)
    weight_specs = (P(), P(), P(None, None, None, "tp", None), P(None, "tp", None, None), P(None, None, "tp"), P(None, "tp", None))

    def device_program(x, ln_gain, ln_bias, w_qkv, w_out, w_up, w_down):
        spatial = local_block(x, ln_gain[0], ln_bias[0], w_qkv[0], w_out[0], w_up[0], w_down[0], SPATIAL_FORMS)
        by_patch = lax.all_to_all(spatial, "sp", 2, 1, tiled=True)
        temporal = local_block(by_patch, ln_gain[1], ln_bias[1], w_qkv[1], w_out[1], w_up[1], w_down[1], TEMPORAL_FORMS)
        return lax.all_to_all(temporal, "sp", 1, 2, tiled=True)

    return jax.shard_map(device_program, mesh=mesh, in_specs=(act_spec,) + weight_specs, out_specs=act_spec, check_vma=False)
```

profile of v0, /device:TPU:1, one launch (start us, length us, event | category | flops | bytes accessed | tf_op | source)
XLA Modules:
  0.0 2640.2 jit_solution(6994025590337784512)
XLA Ops:
  6.5 2.3 convert_reduce_fusion.2
  8.9 2.6 fusion.99
  11.5 0.7 fusion.149
  12.1 0.7 fusion.150
  12.8 2.8 fusion.102
  15.6 0.0 all-gather.5.cloned.1.call-update
  15.6 0.3 reduce-scatter.5.cloned.1.call-start
  16.0 186.3 %all-gather.5.cloned.1.call-done = bf16[1,4,256,5120]{3,2,1,0:T(8,128)(2,1)} async-done(((bf16[1,4,64,5120]{3,2,1,0:T(8,128)(2,1)}), bf16[1,4,256,5120]{3,2,1,0:T(8,128)(2,1)}) %all-gather.5.cloned.1.call-update) | async-done | bytes 10485776 | tf_op jit(solution)/shard_map/all_gather | solution.py:19
  202.2 48.8 %convert_bitcast_fusion.1 = bf16[3,1,4,256,10,128]{5,3,4,0,2,1:T(8,128)(2,1)} fusion(bf16[2,5120,3,10,128]{4,1,3,2,0:T(8,128)(2,1)} %param.10, bf16[1,4,256,5120]{3,2,1,0:T(8,128)(2,1)} %all-gather.5.cloned.1.call-done), kind=kOutput, calls=%fused_computation.65 | convolution fusion | flops 40269250560 | bytes 57671680 | tf_op jit(solution)/shard_map/btsd,dchk->cbtshk/dot_general | solution.py:20
  251.0 4.1 fusion.115
  255.1 4.0 copy-done.6
  259.0 2.7 fusion.151
  261.7 36.7 %fusion.44 = f32[1,4,256,5120]{3,2,1,0:T(8,128)} fusion(bf16[2,10,128,5120]{3,2,1,0:T(8,128)(2,1)} %param.11, f32[4,10,256]{2,1,0:T(8,128)S(1)} %fusion.151, bf16[3,1,4,256,10,128]{5,3,4,0,2,1:T(8,128)(2,1)} %convert_bitcast_fusion.1, f32[4,10,256,256]{2,3,1,0:T(8,128)} %copy-done.6), kind=kOutput, calls=%fused_computation.48 | convolution fusion | flops 14107289600 | bytes 57712640 | tf_op jit(solution)/shard_map/btshk,hkd->btsd/dot_general | solution.py:24
  298.4 0.0 reduce-scatter.5.cloned.1.call-update
  298.5 0.0 all-gather.7.cloned.1.call-start
  298.5 343.8 %reduce-scatter.5.cloned.1.call-done = f32[1,4,64,5120]{3,2,1,0:T(8,128)} async-done(((f32[1,4,256,5120]{3,2,1,0:T(8,128)}), f32[1,4,64,5120]{3,2,1,0:T(8,128)}) %reduce-scatter.5.cloned.1.call-update) | async-done | bytes 5242896 | tf_op jit(solution)/shard_map/reduce_scatter | solution.py:25
  642.3 3.4 convert_reduce_fusion.1
  645.7 0.0 copy-start.4
  645.7 0.8 fusion.95
  646.6 0.6 copy-done.4
  647.2 2.8 fusion.98
  650.0 0.0 all-gather.7.cloned.1.call-update
  650.0 0.0 reduce-scatter.7.cloned.1.call-start
  650.1 186.0 %all-gather.7.cloned.1.call-done = bf16[1,4,256,5120]{3,2,1,0:T(8,128)(2,1)} async-done(((bf16[1,4,64,5120]{3,2,1,0:T(8,128)(2,1)}), bf16[1,4,256,5120]{3,2,1,0:T(8,128)(2,1)}) %all-gather.7.cloned.1.call-update) | async-done | bytes 10485776 | tf_op jit(solution)/shard_map/all_gather | solution.py:27
  836.1 44.8 %fusion.55 = bf16[4,256,3456]{2,1,0:T(8,128)(2,1)S(1)} fusion(bf16[2,5120,3456]{2,1,0:T(8,128)(2,1)} %param.12, bf16[1,4,256,5120]{3,2,1,0:T(8,128)(2,1)} %all-gather.7.cloned.1.call-done), kind=kOutput, calls=%fused_computation.69 | convolution fusion | flops 36242325504 | bytes 52953088 | tf_op jit(solution)/shard_map/btsd,df->btsf/dot_general | solution.py:28
  880.9 50.4 %fusion.38 = f32[1,4,256,5120]{3,2,1,0:T(8,128)} fusion(bf16[2,3456,5120]{2,1,0:T(8,128)(2,1)} %param.13, bf16[4,256,3456]{2,1,0:T(8,128)(2,1)S(1)} %fusion.55), kind=kOutput, calls=%fused_computation.46 | convolution fusion | flops 36274176000 | bytes 63438848 | tf_op jit(solution)/shard_map/btsf,fd->btsd/dot_general | solution.py:30
  931.3 0.0 reduce-scatter.7.cloned.1.call-update
  931.3 0.3 all-gather.9.cloned.1.call-start
  931.6 343.6 %reduce-scatter.7.cloned.1.call-done = f32[1,4,64,5120]{3,2,1,0:T(8,128)} async-done(((f32[1,4,256,5120]{3,2,1,0:T(8,128)}), f32[1,4,64,5120]{3,2,1,0:T(8,128)}) %reduce-scatter.7.cloned.1.call-update) | async-done | bytes 5242896 | tf_op jit(solution)/shard_map/reduce_scatter | solution.py:31
  1275.2 3.2 fusion.104
  1278.4 2.0 copy.23
  1280.4 34.1 %all_to_all.27 = bf16[1,4,64,5120]{3,1,0,2:T(4,128)(2,1)S(1)} all-to-all(bf16[1,4,64,5120]{3,1,0,2:T(4,128)(2,1)S(1)} %copy.23), channel_id=1, replica_groups=mesh['data'=2,'tp'=4,'sp'=4] {'sp'}, dimensions={2} | all-to-all | bytes 5242880 | tf_op jit(solution)/shard_map/all_to_all | solution.py:41
  1314.5 0.7 convert.5
  1315.2 0.9 copy.24
  1316.1 2.8 bitcast_reduce_fusion
  1318.9 2.8 fusion.107
  1321.7 2.6 add_convert_fusion.1
  1324.4 0.0 all-gather.9.cloned.1.call-update
  1324.4 0.4 reduce-scatter.9.cloned.1.call-start
  1324.9 184.5 %all-gather.9.cloned.1.call-done = bf16[1,16,64,5120]{3,2,1,0:T(8,128)(2,1)} async-done(((bf16[1,16,16,5120]{3,2,1,0:T(8,128)(2,1)}), bf16[1,16,64,5120]{3,2,1,0:T(8,128)(2,1)}) %all-gather.9.cloned.1.call-update) | async-done | bytes 10485776 | tf_op jit(solution)/shard_map/all_gather | solution.py:19
  1509.3 47.6 %convert_bitcast_fusion = bf16[3,1,16,64,10,128]{5,3,4,0,2,1:T(8,128)(2,1)S(1)} fusion(bf16[2,5120,3,10,128]{4,1,3,2,0:T(8,128)(2,1)} %param.10, bf16[1,16,64,5120]{3,2,1,0:T(8,128)(2,1)} %all-gather.9.cloned.1.call-done), kind=kOutput, calls=%fused_computation.61 | convolution fusion | flops 40269250560 | bytes 57671680 | tf_op jit(solution)/shard_map/btsd,dchk->cbtshk/dot_general | solution.py:20
  1557.0 2.0 slice_bitcast_fusion.2
  1559.0 10.4 fusion.119
  1569.4 20.4 fusion.152
  1589.8 6.2 convert_bitcast_fusion.2
  1596.0 19.8 fusion.47
  1615.8 0.0 reduce-scatter.9.cloned.1.call-update
  1615.8 0.0 all-gather.11.cloned.1.call-start
  1615.9 343.8 %reduce-scatter.9.cloned.1.call-done = f32[1,16,16,5120]{3,2,1,0:T(8,128)} async-done(((f32[1,16,64,5120]{3,2,1,0:T(8,128)}), f32[1,16,16,5120]{3,2,1,0:T(8,128)}) %reduce-scatter.9.cloned.1.call-update) | async-done | bytes 5242896 | tf_op jit(solution)/shard_map/reduce_scatter | solution.py:25
  1959.7 4.9 convert_reduce_fusion
  1964.6 0.0 copy-start.2
  1964.6 0.8 fusion.91
  1965.4 0.7 copy-done.2
  1966.1 2.8 fusion.94
  1968.9 0.0 all-gather.11.cloned.1.call-update
  1968.9 0.0 reduce-scatter.11.cloned.1.call-start
  1969.0 186.1 %all-gather.11.cloned.1.call-done = bf16[1,16,64,5120]{3,2,1,0:T(8,128)(2,1)} async-done(((bf16[1,16,16,5120]{3,2,1,0:T(8,128)(2,1)}), bf16[1,16,64,5120]{3,2,1,0:T(8,128)(2,1)}) %all-gather.11.cloned.1.call-update) | async-done | bytes 10485776 | tf_op jit(solution)/shard_map/all_gather | solution.py:27
  2155.1 44.8 %fusion.60 = bf16[16,64,3456]{2,1,0:T(8,128)(2,1)S(1)} fusion(bf16[2,5120,3456]{2,1,0:T(8,128)(2,1)} %param.12, bf16[1,16,64,5120]{3,2,1,0:T(8,128)(2,1)} %all-gather.11.cloned.1.call-done), kind=kOutput, calls=%fused_computation.70 | convolution fusion | flops 36242325504 | bytes 52953088 | tf_op jit(solution)/shard_map/btsd,df->btsf/dot_general | solution.py:28
  2199.9 50.3 %fusion.41 = f32[1,16,64,5120]{3,2,1,0:T(8,128)} fusion(bf16[2,3456,5120]{2,1,0:T(8,128)(2,1)} %param.13, bf16[16,64,3456]{2,1,0:T(8,128)(2,1)S(1)} %fusion.60), kind=kOutput, calls=%fused_computation.47 | convolution fusion | flops 36274176000 | bytes 63438848 | tf_op jit(solution)/shard_map/btsf,fd->btsd/dot_general | solution.py:30
  2250.2 0.0 reduce-scatter.11.cloned.1.call-update
  2250.2 343.9 %reduce-scatter.11.cloned.1.call-done = f32[1,16,16,5120]{3,2,1,0:T(8,128)} async-done(((f32[1,16,64,5120]{3,2,1,0:T(8,128)}), f32[1,16,16,5120]{3,2,1,0:T(8,128)}) %reduce-scatter.11.cloned.1.call-update) | async-done | bytes 5242896 | tf_op jit(solution)/shard_map/reduce_scatter | solution.py:31
  2594.1 3.2 fusion.114
  2597.3 34.1 %all_to_all.28 = bf16[1,16,16,5120]{3,2,0,1:T(8,128)(2,1)S(1)} all-to-all(bf16[1,16,16,5120]{3,2,0,1:T(8,128)(2,1)S(1)} %fusion.114), channel_id=1, replica_groups=mesh['data'=2,'tp'=4,'sp'=4] {'sp'}, dimensions={1} | all-to-all | bytes 5242880 | tf_op jit(solution)/shard_map/all_to_all | solution.py:43
  2631.4 1.7 copy.31
  (30 shorter events, 0.1 us)
Async XLA Ops:
  6.5 6.3 copy-start.1
  6.5 4.9 copy-start.9
  6.5 5.6 copy-start.10
  6.5 195.7 %all-gather.5.cloned.1.call-start = ((), (), s32[]{:S(2)}) async-start(), calls=%async_computation.6 | async-start | bytes 13107200 | tf_op jit(solution)/shard_map/all_gather | solution.py:19
  15.6 626.7 %reduce-scatter.5.cloned.1.call-start = ((), (), s32[]{:S(2)}) async-start(), calls=%async_computation.7 | async-start | bytes 26214400 | tf_op jit(solution)/shard_map/reduce_scatter | solution.py:25
  255.1 4.0 copy-start.6
  298.5 537.7 %all-gather.7.cloned.1.call-start = ((), (), s32[]{:S(2)}) async-start(), calls=%async_computation.8 | async-start | bytes 13107200 | tf_op jit(solution)/shard_map/all_gather | solution.py:27
  645.7 1.5 copy-start.4
  650.0 625.2 %reduce-scatter.7.cloned.1.call-start = ((), (), s32[]{:S(2)}) async-start(), calls=%async_computation.9 | async-start | bytes 26214400 | tf_op jit(solution)/shard_map/reduce_scatter | solution.py:31
  931.3 343.9 %copy-start.5 = (bf16[1,4,64,5120]{3,2,1,0:T(8,128)(2,1)S(1)}, bf16[1,4,64,5120]{3,2,1,0:T(8,128)(2,1)}, u32[]{:S(2)}) copy-start(bf16[1,4,64,5120]{3,2,1,0:T(8,128)(2,1)} %copy-done.4) | copy-start | bytes 7864324
  931.3 578.0 %all-gather.9.cloned.1.call-start = ((), (), s32[]{:S(2)}) async-start(), calls=%async_computation.10 | async-start | bytes 13107200 | tf_op jit(solution)/shard_map/all_gather | solution.py:19
  1316.1 5.6 copy-start
  1316.1 5.6 copy-start.7
  1316.1 5.6 copy-start.8
  1324.4 635.3 %reduce-scatter.9.cloned.1.call-start = ((), (), s32[]{:S(2)}) async-start(), calls=%async_computation.11 | async-start | bytes 26214400 | tf_op jit(solution)/shard_map/reduce_scatter | solution.py:25
  1615.8 350.3 %copy-start.11 = (f32[1,1,5120]{2,1,0:T(1,128)S(1)}, f32[1,1,5120]{2,1,0:T(1,128)}, u32[]{:S(2)}) copy-start(f32[1,1,5120]{2,1,0:T(1,128)} %get-tuple-element.12) | copy-start | bytes 61444
  1615.8 350.3 %copy-start.12 = (f32[1,1,5120]{2,1,0:T(1,128)S(1)}, f32[1,1,5120]{2,1,0:T(1,128)}, u32[]{:S(2)}) copy-start(f32[1,1,5120]{2,1,0:T(1,128)} %get-tuple-element.16) | copy-start | bytes 61444
  1615.8 539.2 %all-gather.11.cloned.1.call-start = ((), (), s32[]{:S(2)}) async-start(), calls=%async_computation.12 | async-start | bytes 13107200 | tf_op jit(solution)/shard_map/all_gather | solution.py:27
  1964.6 1.5 copy-start.2
  1968.9 625.2 %reduce-scatter.11.cloned.1.call-start = ((), (), s32[]{:S(2)}) async-start(), calls=%async_computation.13 | async-start | bytes 26214400 | tf_op jit(solution)/shard_map/reduce_scatter | solution.py:31
  2250.2 343.9 %copy-start.3 = (bf16[1,16,16,5120]{3,2,1,0:T(8,128)(2,1)S(1)}, bf16[1,16,16,5120]{3,2,1,0:T(8,128)(2,1)}, u32[]{:S(2)}) copy-start(bf16[1,16,16,5120]{3,2,1,0:T(8,128)(2,1)} %copy-done.2) | copy-start | bytes 7864324
Sparse Core Ops, SparseCore 0:
  15.7 186.4 all-gather.4
  298.6 343.7 reduce-scatter.4
  650.1 185.9 all-gather.6
  931.4 343.7 reduce-scatter.6
  1324.5 184.7 all-gather.8
  1615.9 343.7 reduce-scatter.8
  1969.0 185.9 all-gather.10
  2250.4 343.7 reduce-scatter.10
where the time goes:
time: 2640 us
  waiting for transfers between devices  2120 us (80%)
  matrix products  364 us (14%)
  blocking collectives  68.2 us (3%)
  other arithmetic  61.6 us (2%)
    reduce_scatter x2, waiting for transfers between devices, local_block(): lax.psum_scatter(part_sum, 'tp', scatter_dimension=2, tiled=True)  688 us
    reduce_scatter x2, waiting for transfers between devices, local_block(): lax.psum_scatter(part_down, 'tp', scatter_dimension=2, tiled=True)  687 us
    all_gather x2, waiting for transfers between devices, local_block(): lax.all_gather(layer_norm(hidden, gain[1], shift[1]), 'tp', axis=2, tiled...  372 us
    all_gather x2, waiting for transfers between devices, local_block(): lax.all_gather(layer_norm(residual, gain[0], shift[0]), 'tp', axis=2, til...  371 us
    dot_general x2, matrix products, local_block(): jnp.einsum('btsf,fd->btsd', gelu_out, w_down, preferred_element_type=jnp....  101 us
    dot_general x2, matrix products, local_block(): jnp.einsum('btsd,dchk->cbtshk', gathered, w_qkv, preferred_element_type=j...  96.4 us
    dot_general x2, matrix products, local_block(): jnp.einsum('btsd,df->btsf', gathered_mlp, w_up, preferred_element_type=jn...  89.6 us
    dot_general x2, matrix products, local_block(): jnp.einsum('btshk,hkd->btsd', mixed, w_out, preferred_element_type=jnp.fl...  56.5 us
  transfers between devices with their start and end apart: 8, of which 8 were waited for; matrix products, arithmetic and copies ran while one was open for 0% of the time, Pallas kernels for 0%

commit v1 on v0

v1 whole, which is shorter than its diff:
```python
import functools

import jax
import jax.numpy as jnp
from jax import lax
from jax.experimental import pallas as pl
from jax.experimental.pallas import tpu as pltpu
from jax.sharding import PartitionSpec as P

bf16, f32 = jnp.bfloat16, jnp.float32
MESH = pl.DeviceIdType.MESH
LINE = 4
NB = 256
UB = 384
RB = 16
VMEM_LIMIT = 66_500_000


def shift(axis_bits):
    data, sp = lax.axis_index("data"), lax.axis_index("sp")
    fx, fy, fc = axis_bits
    data = 1 - data if fx else data
    y, core = sp // 2, sp % 2
    y = 1 - y if fy else y
    core = 1 - core if fc else core
    return {"data": data, "sp": y * 2 + core}


PEERS = ((0, 0, 1), (0, 1, 0), (1, 0, 0), (1, 1, 0))


class Line:
    def __init__(self):
        self.z = lax.axis_index("tp")

    def exists(self, direction):
        return self.z < LINE - 1 if direction == 0 else self.z > 0

    def source_exists(self, direction):
        return self.z > 0 if direction == 0 else self.z < LINE - 1

    def target(self, direction):
        return {"tp": self.z + 1 if direction == 0 else self.z - 1}

    def origin(self, direction, hop):
        return self.z - hop if direction == 0 else self.z + hop

    def sends(self, direction, hop):
        o = self.origin(direction, hop)
        return jnp.logical_and(self.exists(direction), jnp.logical_and(o >= 0, o < LINE))

    def receives(self, direction, hop):
        o = self.origin(direction, hop + 1)
        return jnp.logical_and(o >= 0, o < LINE)


def remote(src, dst, send, recv, device):
    return pltpu.make_async_remote_copy(src_ref=src, dst_ref=dst, send_sem=send, recv_sem=recv, device_id=device, device_id_type=MESH)


class Gather:
    def __init__(self, line, own, slot, send, recv):
        self.line, self.own, self.slot, self.send, self.recv = line, own, slot, send, recv

    def copy(self, d, c, hop):
        o = jnp.clip(self.line.origin(d, hop), 0, LINE - 1)
        src = self.own(c) if hop == 0 else self.slot(c, o)
        return remote(src, self.slot(c, o), self.send.at[d, c, hop], self.recv.at[d, c, hop], self.line.target(d))

    def arrival(self, d, c, hop):
        o = jnp.clip(self.line.origin(d, hop + 1), 0, LINE - 1)
        here = self.slot(c, o)
        return remote(here, here, self.send.at[d, c, hop], self.recv.at[d, c, hop], self.line.target(d))

    def start(self, c, hop):
        for d in range(2):
            @pl.when(self.line.sends(d, hop))
            def _():
                self.copy(d, c, hop).start()

    def arrive(self, c, hop):
        for d in range(2):
            @pl.when(self.line.receives(d, hop))
            def _():
                self.arrival(d, c, hop).wait_recv()

    def relay(self, c, hop):
        self.arrive(c, hop - 1)
        self.start(c, hop)

    def finish(self, chunks):
        for c in range(chunks):
            for hop in range(LINE - 1):
                for d in range(2):
                    @pl.when(self.line.sends(d, hop))
                    def _():
                        self.copy(d, c, hop).wait_send()


def meet(line, peers):
    barrier = pltpu.get_barrier_semaphore()
    for d in range(2):
        @pl.when(line.exists(d))
        def _():
            pl.semaphore_signal(barrier, inc=1, device_id=line.target(d), device_id_type=MESH)
    for p in peers:
        pl.semaphore_signal(barrier, inc=1, device_id=shift(p), device_id_type=MESH)
    pl.semaphore_wait(barrier, jnp.where(jnp.logical_or(line.z == 0, line.z == LINE - 1), 1, 2) + len(peers))


def normalize(src, dst, gain, bias):
    def rows(i, _):
        at = pl.ds(pl.multiple_of(i * RB, RB), RB)
        u = src[at, :].astype(f32)
        u = u - jnp.mean(u, axis=-1, keepdims=True)
        var = jnp.mean(u * u, axis=-1, keepdims=True)
        dst[at, :] = (u * lax.rsqrt(var + 1e-6) * gain[...] + bias[...]).astype(bf16)
        return 0

    lax.fori_loop(0, src.shape[0] // RB, rows, 0)


def tiles(count, copies, compute):
    for when, copy in copies(0, 0):
        when(copy.start) if when else copy.start()

    def step(n, _):
        slot = lax.rem(n, 2)

        @pl.when(n + 1 < count)
        def _():
            for when, copy in copies(n + 1, 1 - slot):
                when(copy.start) if when else copy.start()

        for when, copy in copies(n, slot):
            when(copy.wait) if when else copy.wait()
        compute(n, slot)
        return 0

    lax.fori_loop(0, count, step, 0)


def gather_attend(cfg, b, x, gain, bias, wq, wo, r_out, o_out, wg, rv, nv, wbuf, qkv, ov, xs, xr, ws, wr, ps, pr, fs, fr, ls, ts):
    chunks, rows, width = x.shape
    tokens = rows * LINE
    hk = wo.shape[1]
    heads = hk // 128
    cols = width // 8
    line = Line()
    z = line.z
    place = lax.axis_index("data") * 4 + lax.axis_index("sp")
    at_cols = lambda p: pl.ds(pl.multiple_of(p * cols, 128), cols)
    g = Gather(line, lambda c: x.at[c], lambda c, o: r_out.at[c, o], xs, xr)
    w = Gather(line, lambda c: wo.at[b, :, at_cols(place)], lambda c, o: wg.at[o, :, at_cols(place)], ws, wr)

    def peer_place(k):
        dev = shift(PEERS[k])
        return dev["data"] * 4 + dev["sp"]

    def plane(d, hop, k, p):
        o = jnp.clip(line.origin(d, hop + 1), 0, LINE - 1)
        return wg.at[o, :, at_cols(p)]

    def spread(hop):
        for d in range(2):
            @pl.when(line.receives(d, hop))
            def _():
                for k in range(4):
                    ref = plane(d, hop, k, place)
                    remote(ref, ref, ps.at[d, hop, k], pr.at[d, hop, k], shift(PEERS[k])).start()

    def forward(hop):
        for d in range(2):
            @pl.when(line.receives(d, hop))
            def _():
                for k in range(1, 4):
                    ref = plane(d, hop, k, peer_place(k))
                    remote(ref, ref, ps.at[d, hop, k], pr.at[d, hop, k], shift(PEERS[k])).wait_recv()
                    remote(ref, ref, fs.at[d, hop, k - 1], fr.at[d, hop, k - 1], shift(PEERS[0])).start()

    def plane_finish():
        for hop in range(LINE - 1):
            for d in range(2):
                @pl.when(line.receives(d, hop))
                def _():
                    for k in range(4):
                        ref = plane(d, hop, k, place)
                        remote(ref, ref, ps.at[d, hop, k], pr.at[d, hop, k], shift(PEERS[k])).wait_send()
                    ref = plane(d, hop, 0, peer_place(0))
                    remote(ref, ref, ps.at[d, hop, 0], pr.at[d, hop, 0], shift(PEERS[0])).wait_recv()
                    for k in range(1, 4):
                        ref = plane(d, hop, k, peer_place(k))
                        remote(ref, ref, fs.at[d, hop, k - 1], fr.at[d, hop, k - 1], shift(PEERS[0])).wait_send()
                        far = shift(tuple(m ^ n for m, n in zip(PEERS[k], PEERS[0])))
                        ref = plane(d, hop, k, far["data"] * 4 + far["sp"])
                        remote(ref, ref, fs.at[d, hop, k - 1], fr.at[d, hop, k - 1], shift(PEERS[0])).wait_recv()

    def load(c):
        copies = []
        for s in range(LINE):
            there = rv.at[pl.ds(s * rows, rows), :]
            copies.append((z == s, pltpu.make_async_copy(x.at[c], there, ls.at[s]), pltpu.make_async_copy(r_out.at[c, s], there, ls.at[s])))
        for mine, a, o in copies:
            pl.when(mine)(a.start)
            pl.when(jnp.logical_not(mine))(o.start)
        for _, a, _ in copies:
            a.wait()

    def own_rows(c):
        at = pl.ds(pl.multiple_of(z * rows, rows), rows)
        return pltpu.make_async_copy(rv.at[at, :], r_out.at[c, z], ls.at[LINE])

    def work(c):
        g.arrive(c, 2)
        load(c)
        own_rows(c).start()
        normalize(rv, nv, gain, bias)
        pairs = heads // 2

        def copies(n, slot):
            part, pair = n // pairs, n % pairs
            return [(None, pltpu.make_async_copy(wq.at[b, part, pair * 2 + i], wbuf.at[slot, :, pl.ds(i * 128, 128)], ts.at[slot, i])) for i in range(2)]

        def compute(n, slot):
            at = pl.ds(pl.multiple_of(n * NB, NB), NB)
            qkv[:, at] = jnp.dot(nv[...], wbuf[slot], preferred_element_type=f32).astype(bf16)

        tiles(3 * pairs, copies, compute)
        if cfg["step"]:
            step = cfg["step"]
            key = lambda t: t // rows * step + t % step
            mask = key(lax.broadcasted_iota(jnp.int32, (tokens, tokens), 0)) == key(lax.broadcasted_iota(jnp.int32, (tokens, tokens), 1))

        def head(h, _):
            at = lambda part: pl.ds(pl.multiple_of((part * heads + h) * 128, 128), 128)
            s = lax.dot_general(qkv[:, at(0)], qkv[:, at(1)], (((1,), (1,)), ((), ())), preferred_element_type=f32) * 128**-0.5
            if cfg["step"]:
                s = jnp.where(mask, s, -1e30)
            e = jnp.exp(s - jnp.max(s, axis=-1, keepdims=True))
            p = (e * (1.0 / jnp.sum(e, axis=-1, keepdims=True))).astype(bf16)
            ov[:, pl.ds(pl.multiple_of(h * 128, 128), 128)] = jnp.dot(p, qkv[:, at(2)], preferred_element_type=f32).astype(bf16)
            return 0

        lax.fori_loop(0, heads, head, 0)
        out = pltpu.make_async_copy(ov, o_out.at[c], ls.at[LINE + 1])
        out.start()
        own_rows(c).wait()
        out.wait()

    meet(line, PEERS)
    w.start(0, 0)
    g.start(0, 0)
    w.relay(0, 1)
    spread(0)
    g.start(1, 0)
    g.relay(0, 1)
    g.start(2, 0)
    w.relay(0, 2)
    spread(1)
    g.relay(0, 2)
    g.relay(1, 1)
    g.start(3, 0)
    w.arrive(0, 2)
    spread(2)
    g.relay(1, 2)
    g.relay(2, 1)
    work(0)
    g.relay(2, 2)
    g.relay(3, 1)
    work(1)
    g.relay(3, 2)
    forward(0)
    work(2)
    forward(1)
    work(3)
    forward(2)
    g.finish(chunks)
    w.finish(1)
    plane_finish()


def mix_feed(b, o, r, wo, wg, gain, bias, wu, wd, y, og, part, rv, nv, gv, mine, wbuf, got, add, pst, os_, or_, rs, rr, ls, ts, ds):
    chunks, tokens, hk = o.shape
    rows = tokens // LINE
    width, hidden = wu.shape[1:]
    line = Line()
    z = line.z
    g = Gather(line, lambda c: o.at[c], lambda c, s: og.at[c, s], os_, or_)

    def out_copies(n, slot):
        cols = pl.ds(pl.multiple_of(n * NB, NB), NB)
        copies = []
        for s in range(LINE):
            there = wbuf.at[slot, pl.ds(s * hk, hk), pl.ds(0, NB)]
            copies.append((pl.when(z == s), pltpu.make_async_copy(wo.at[b, :, cols], there, ts.at[slot, s])))
            copies.append((pl.when(z != s), pltpu.make_async_copy(wg.at[s, :, cols], there, ts.at[slot, s])))
        return copies

    def load(c):
        copies = [pltpu.make_async_copy(r.at[c], rv, ls.at[LINE])]
        for c_ in copies:
            c_.start()
        both = []
        for s in range(LINE):
            there = nv.at[:, pl.ds(s * hk, hk)]
            both.append((z == s, pltpu.make_async_copy(o.at[c], there, ls.at[s]), pltpu.make_async_copy(og.at[c, s], there, ls.at[s])))
        for own, a, other in both:
            pl.when(own)(a.start)
            pl.when(jnp.logical_not(own))(other.start)
        for _, a, _ in both:
            a.wait()
        copies[0].wait()

    def project(c):
        load(c)

        def compute(n, slot):
            at = pl.ds(pl.multiple_of(n * NB, NB), NB)
            a = jnp.dot(nv[...], wbuf[slot, :, :NB], preferred_element_type=f32).astype(bf16)
            rv[:, at] = (rv[:, at].astype(f32) + a.astype(f32)).astype(bf16)

        tiles(width // NB, out_copies, compute)
        normalize(rv, nv, gain, bias)
        mine[c] = rv[pl.ds(pl.multiple_of(z * rows, rows), rows), :]

    def up(c):
        def copies(n, slot):
            cols = pl.ds(pl.multiple_of(n * UB, 128), UB)
            return [(None, pltpu.make_async_copy(wu.at[b, :, cols], wbuf.at[slot], ts.at[slot, 0]))]

        def compute(n, slot):
            u = jnp.dot(nv[...], wbuf[slot], preferred_element_type=f32).astype(bf16).astype(f32)
            gv[:, pl.ds(pl.multiple_of(n * UB, 128), UB)] = jax.nn.gelu(u, approximate=True).astype(bf16)

        tiles(hidden // UB, copies, compute)

    def store(c, n, slot):
        cols = pl.ds(pl.multiple_of(n * NB, NB), NB)
        return pltpu.make_async_copy(pst.at[slot], part.at[c, :, cols], ds.at[slot])

    def down(c):
        count = width // NB

        def copies(n, slot):
            cols = pl.ds(pl.multiple_of(n * NB, NB), NB)
            return [(None, pltpu.make_async_copy(wd.at[b, :, cols], wbuf.at[slot, pl.ds(0, hidden), pl.ds(0, NB)], ts.at[slot, 0]))]

        def compute(n, slot):
            @pl.when(n >= 2)
            def _():
                store(c, n - 2, slot).wait()

            pst[slot] = jnp.dot(gv[...], wbuf[slot, :hidden, :NB], preferred_element_type=f32)
            store(c, n, slot).start()

        tiles(count, copies, compute)
        for n in (count - 2, count - 1):
            store(c, n, n % 2).wait()

    def term(c, t):
        return part.at[c, pl.ds(pl.multiple_of(t * rows, rows), rows), :]

    def hop_copy(d, c, far, src):
        return remote(src, got.at[d, c, LINE - 1 - far], rs.at[d, c, LINE - 1 - far], rr.at[d, c, LINE - 1 - far], line.target(d))

    def first(d):
        return z == 0 if d == 0 else z == LINE - 1

    def far_target(d, far):
        return z + far if d == 0 else z - far

    def reduce_start(c):
        for far in range(LINE - 1, 0, -1):
            for d in range(2):
                @pl.when(first(d))
                def _():
                    hop_copy(d, c, far, term(c, far if d == 0 else LINE - 1 - far)).start()

    def middle(d, far):
        t = far_target(d, far - 1)
        return jnp.logical_and(jnp.logical_not(first(d)), jnp.logical_and(t >= 0, t < LINE))

    def reduce_relay(c, far):
        for d in range(2):
            @pl.when(middle(d, far))
            def _():
                t = jnp.clip(far_target(d, far - 1), 0, LINE - 1)
                fetch = pltpu.make_async_copy(term(c, t), add, ls.at[LINE + 1])
                fetch.start()
                slot = got.at[d, c, LINE - 1 - far]
                hop_copy(d, c, far, slot).wait_recv()
                fetch.wait()

                def some(i, _):
                    at = pl.ds(pl.multiple_of(i * RB, RB), RB)
                    slot[at, :] = slot[at, :] + add[at, :]
                    return 0

                lax.fori_loop(0, rows // RB, some, 0)
                hop_copy(d, c, far - 1, slot).start()

    def result(c):
        return pltpu.make_async_copy(mine.at[c], y.at[c], ls.at[LINE + 2])

    def reduce_finish(c):
        fetch = pltpu.make_async_copy(term(c, z), add, ls.at[LINE + 1])
        fetch.start()
        for d in range(2):
            @pl.when(jnp.logical_not(first(d)))
            def _():
                hop_copy(d, c, 1, got.at[d, c, LINE - 2]).wait_recv()
        fetch.wait()

        def some(i, _):
            at = pl.ds(pl.multiple_of(i * RB, RB), RB)
            for d in range(2):
                @pl.when(jnp.logical_not(first(d)))
                def _():
                    add[at, :] = add[at, :] + got[d, c, LINE - 2, at, :]
            m = add[at, :].astype(bf16)
            mine[c, at, :] = (mine[c, at, :].astype(f32) + m.astype(f32)).astype(bf16)
            return 0

        lax.fori_loop(0, rows // RB, some, 0)
        result(c).start()
        result(c).wait()

    def reduce_sent(c):
        for far in range(LINE - 1, 0, -1):
            for d in range(2):
                @pl.when(first(d))
                def _():
                    hop_copy(d, c, far, term(c, 0)).wait_send()
                if far > 1:
                    @pl.when(middle(d, far))
                    def _():
                        hop_copy(d, c, far - 1, got.at[d, c, LINE - 1 - far]).wait_send()

    meet(line, ())
    g.start(0, 0)
    g.relay(0, 1)
    g.start(1, 0)
    g.relay(0, 2)
    g.relay(1, 1)
    g.start(2, 0)
    g.arrive(0, 2)
    project(0)
    g.relay(1, 2)
    g.relay(2, 1)
    g.start(3, 0)
    up(0)
    g.relay(2, 2)
    g.relay(3, 1)
    down(0)
    reduce_start(0)
    g.relay(3, 2)
    g.arrive(1, 2)
    project(1)
    up(1)
    reduce_relay(0, 3)
    down(1)
    reduce_start(1)
    reduce_relay(0, 2)
    g.arrive(2, 2)
    project(2)
    reduce_finish(0)
    up(2)
    down(2)
    reduce_start(2)
    reduce_relay(1, 3)
    reduce_relay(1, 2)
    g.arrive(3, 2)
    project(3)
    up(3)
    reduce_finish(1)
    down(3)
    reduce_start(3)
    reduce_relay(2, 3)
    reduce_relay(2, 2)
    reduce_finish(2)
    reduce_relay(3, 3)
    reduce_relay(3, 2)
    reduce_finish(3)
    g.finish(chunks)
    for c in range(chunks):
        reduce_sent(c)


ANY = pl.BlockSpec(memory_space=pl.ANY)
VMEM = pl.BlockSpec(memory_space=pltpu.VMEM)
DMA = pltpu.SemaphoreType.DMA


def call_gather_attend(b, step, x, gain, bias, wq, wo):
    chunks, rows, width = x.shape
    hk, tokens = wo.shape[1], rows * LINE
    hops = LINE - 1
    return pl.pallas_call(
        functools.partial(gather_attend, {"step": step}, b),
        out_shape=(
            jax.ShapeDtypeStruct((chunks, LINE, rows, width), bf16),
            jax.ShapeDtypeStruct((chunks, tokens, hk), bf16),
            jax.ShapeDtypeStruct((LINE, hk, width), bf16),
        ),
        in_specs=[ANY, VMEM, VMEM, ANY, ANY],
        out_specs=(ANY, ANY, ANY),
        scratch_shapes=[
            pltpu.VMEM((tokens, width), bf16), pltpu.VMEM((tokens, width), bf16), pltpu.VMEM((2, width, NB), bf16),
            pltpu.VMEM((tokens, 3 * hk), bf16), pltpu.VMEM((tokens, hk), bf16),
            DMA((2, chunks, hops)), DMA((2, chunks, hops)), DMA((2, 1, hops)), DMA((2, 1, hops)),
            DMA((2, hops, 4)), DMA((2, hops, 4)), DMA((2, hops, 3)), DMA((2, hops, 3)), DMA((LINE + 2,)), DMA((2, 2)),
        ],
        compiler_params=pltpu.CompilerParams(collective_id=b, has_side_effects=True, vmem_limit_bytes=VMEM_LIMIT),
        name=f"gather_attend_{b}",
    )(x, gain, bias, wq, wo)


def call_mix_feed(b, o, r, wo, wg, gain, bias, wu, wd):
    chunks, tokens, hk = o.shape
    rows = tokens // LINE
    width, hidden = wu.shape[1:]
    hops = LINE - 1
    return pl.pallas_call(
        functools.partial(mix_feed, b),
        out_shape=(
            jax.ShapeDtypeStruct((chunks, rows, width), bf16),
            jax.ShapeDtypeStruct((chunks, LINE, tokens, hk), bf16),
            jax.ShapeDtypeStruct((chunks, tokens, width), f32),
        ),
        in_specs=[ANY, ANY, ANY, ANY, VMEM, VMEM, ANY, ANY],
        out_specs=(ANY, ANY, ANY),
        scratch_shapes=[
            pltpu.VMEM((tokens, width), bf16), pltpu.VMEM((tokens, width), bf16), pltpu.VMEM((tokens, hidden), bf16),
            pltpu.VMEM((chunks, rows, width), bf16), pltpu.VMEM((2, width, UB), bf16), pltpu.VMEM((2, chunks, hops, rows, width), f32),
            pltpu.VMEM((rows, width), f32), pltpu.VMEM((2, tokens, NB), f32),
            DMA((2, chunks, hops)), DMA((2, chunks, hops)), DMA((2, chunks, hops)), DMA((2, chunks, hops)),
            DMA((LINE + 3,)), DMA((2, LINE)), DMA((2,)),
        ],
        compiler_params=pltpu.CompilerParams(collective_id=2 + b, has_side_effects=True, vmem_limit_bytes=VMEM_LIMIT),
        name=f"mix_feed_{b}",
    )(o, r, wo, wg, gain, bias, wu, wd)[0]


def solution(mesh):
    act_spec = P("data", "sp", "tp", None)
    weight_specs = (P(), P(), P(None, None, None, "tp", None), P(None, "tp", None, None), P(None, None, "tp"), P(None, "tp", None))

    def device_program(x, ln_gain, ln_bias, w_qkv, w_out, w_up, w_down):
        _, frames, rows, width = x.shape
        wq = w_qkv.transpose(0, 2, 3, 1, 4)
        wo = w_out.reshape(2, -1, width)

        def block(b, r, step):
            row = lambda a, i: a[b, i][None]
            r_full, o, wg = call_gather_attend(b, step, r, row(ln_gain, 0), row(ln_bias, 0), wq, wo)
            r_full = r_full.reshape(r_full.shape[0], -1, width)
            return call_mix_feed(b, o, r_full, wo, wg, row(ln_gain, 1), row(ln_bias, 1), w_up, w_down)

        spatial = block(0, x[0], 0)
        per = rows // 4
        step = per // 4
        turned = lax.all_to_all(spatial, "sp", 1, 0, tiled=True)
        turned = turned.reshape(4 * frames, 4, step, width).transpose(1, 0, 2, 3).reshape(4, -1, width)
        temporal = block(1, turned, step)
        back = temporal.reshape(4, 4 * frames, step, width).transpose(1, 0, 2, 3).reshape(4 * frames, per, width)
        return lax.all_to_all(back, "sp", 0, 1, tiled=True)[None]

    return jax.shard_map(device_program, mesh=mesh, in_specs=(act_spec,) + weight_specs, out_specs=act_spec, check_vma=False)
```

time: 2640 us -> 1860 us (0.70)
  waiting for transfers between devices: 2120 us -> 0 us
  Pallas kernels: 0 us -> 1730 us
  matrix products: 364 us -> 0 us
  other arithmetic: 61.6 us -> 0 us
    pallas_call x0 -> x4, Pallas kernels: none -> 1730 us  [the longest x2 1040 us: call_mix_feed(): pl.pallas_call(functools.partial(mix_feed, b), out_shape=(jax.ShapeDtypeS...]
    reduce_scatter x4 -> x0, waiting for transfers between devices: 1380 us -> none  [the longest x2 688 us: local_block(): lax.psum_scatter(part_sum, 'tp', scatter_dimension=2, tiled=True)]
    all_gather x4 -> x0, waiting for transfers between devices: 743 us -> none  [the longest x2 372 us: local_block(): lax.all_gather(layer_norm(hidden, gain[1], shift[1]), 'tp', axis=2, tiled...]
    dot_general x11 -> x0, matrix products: 364 us -> none  [the longest x2 101 us: local_block(): jnp.einsum('btsf,fd->btsd', gelu_out, w_down, preferred_element_type=jnp....]
  transfers between devices with their start and end apart: 8 -> 0, of which waited for: 8 -> 0; matrix products, arithmetic and copies ran while one was open for 0% -> 0% of each run, Pallas kernels for 0% -> 0%
where the time goes in v1:
time: 1860 us; the launch traced here: 1840 us
  Pallas kernels  1730 us (93%)
  blocking collectives  83.7 us (4%)
  local copies, waits for them, and re-layouts  21.8 us (1%)
    pallas_call x2, Pallas kernels, call_mix_feed(): pl.pallas_call(functools.partial(mix_feed, b), out_shape=(jax.ShapeDtypeS...  1040 us
    pallas_call x2, Pallas kernels, call_gather_attend(): pl.pallas_call(functools.partial(gather_attend, {'step': step}, b), out_s...  699 us
    all_to_all x1, blocking collectives, device_program(): turned = lax.all_to_all(spatial, 'sp', 1, 0, tiled=True)  43.7 us
    all_to_all x1, blocking collectives, device_program(): return lax.all_to_all(back, 'sp', 0, 1, tiled=True)[None]  40 us

profile of v1, /device:TPU:1, one launch (start us, length us, event | category | flops | bytes accessed | tf_op | source)
XLA Modules:
  0.0 1840.9 jit_solution(1057091410059001477)
XLA Ops:
  0.0 1.7 slice_bitcast_fusion
  1.7 349.6 %gather_attend_0.1 = (bf16[4,4,64,5120]{3,2,1,0:T(8,128)(2,1)}, bf16[4,256,1280]{2,1,0:T(8,128)(2,1)}, bf16[4,1280,5120]{2,1,0:T(8,128)(2,1)}) custom-call(bf16[4,64,5120]{2,1,0:T(8,128)(2,1)} %bitcast.46, f32[1,5120]{1,0:T(1,128)} %get-tuple-element.30.gain, f32[1,5120]{1,0:T(1,128)} %get-tuple-element.23.bias, bf16[2,3,10,5120,128]{4,3,2,1,0:T(8,128)(2,1)} %bitcast.3.wq, ...), custom_call_target="tpu_custom_call" | custom-call | tf_op jit(solution)/shard_map/gather_attend_0/pallas_call | solution.py:498
  351.3 515.4 %mix_feed_0.1 = (bf16[4,64,5120]{2,1,0:T(8,128)(2,1)}, bf16[4,4,256,1280]{3,2,1,0:T(8,128)(2,1)}, f32[4,256,5120]{2,1,0:T(8,128)}) custom-call(bf16[4,256,1280]{2,1,0:T(8,128)(2,1)} %get-tuple-element.13.o, bf16[4,256,5120]{2,1,0:T(8,128)(2,1)} %bitcast.40, bf16[2,1280,5120]{2,1,0:T(8,128)(2,1)} %bitcast.36, bf16[4,1280,5120]{2,1,0:T(8,128)(2,1)} %get-tuple-element.15.wg, ...), custom_call_target="tpu_custom_call" | custom-call | tf_op jit(solution)/shard_map/mix_feed_0/pallas_call | solution.py:523
  866.7 3.8 copy.17
  870.5 43.7 %all_to_all.30 = bf16[4,64,5120]{2,0,1:T(4,128)(2,1)S(1)} all-to-all(bf16[4,64,5120]{2,0,1:T(4,128)(2,1)S(1)} %copy.17), channel_id=1, replica_groups=mesh['data'=2,'tp'=4,'sp'=4] {'sp'}, dimensions={1} | all-to-all | bytes 5242880 | tf_op jit(solution)/shard_map/all_to_all | solution.py:562
  914.2 0.8 copy.24
  915.0 2.4 reshape.25
  917.4 2.7 copy.19
  920.1 2.2 reshape.26.x
  922.3 349.8 %gather_attend_1.1 = (bf16[4,4,64,5120]{3,2,1,0:T(8,128)(2,1)}, bf16[4,256,1280]{2,1,0:T(8,128)(2,1)}, bf16[4,1280,5120]{2,1,0:T(8,128)(2,1)}) custom-call(bf16[4,64,5120]{2,1,0:T(8,128)(2,1)} %reshape.26.x, f32[1,5120]{1,0:T(1,128)} %get-tuple-element.29.gain, f32[1,5120]{1,0:T(1,128)} %get-tuple-element.24.bias, bf16[2,3,10,5120,128]{4,3,2,1,0:T(8,128)(2,1)} %bitcast.3.wq, ...), custom_call_target="tpu_custom_call" | custom-call | tf_op jit(solution)/shard_map/gather_attend_1/pallas_call | solution.py:498
  1272.1 520.0 %mix_feed_1.1 = (bf16[4,64,5120]{2,1,0:T(8,128)(2,1)}, bf16[4,4,256,1280]{3,2,1,0:T(8,128)(2,1)}, f32[4,256,5120]{2,1,0:T(8,128)}) custom-call(bf16[4,256,1280]{2,1,0:T(8,128)(2,1)} %get-tuple-element.17.o, bf16[4,256,5120]{2,1,0:T(8,128)(2,1)} %bitcast.39, bf16[2,1280,5120]{2,1,0:T(8,128)(2,1)} %bitcast.38, bf16[4,1280,5120]{2,1,0:T(8,128)(2,1)} %get-tuple-element.19.wg, ...), custom_call_target="tpu_custom_call" | custom-call | tf_op jit(solution)/shard_map/mix_feed_1/pallas_call | solution.py:523
  1792.1 4.3 reshape.28
  1796.4 0.8 copy.20
  1797.2 1.4 copy.21
  1798.6 40.0 %all_to_all.31 = bf16[16,16,5120]{2,1,0:T(8,128)(2,1)S(1)} all-to-all(bf16[16,16,5120]{2,1,0:T(8,128)(2,1)S(1)} %copy.21), channel_id=1, replica_groups=mesh['data'=2,'tp'=4,'sp'=4] {'sp'}, dimensions={0} | all-to-all | bytes 5242880 | tf_op jit(solution)/shard_map/all_to_all | solution.py:566
  1838.7 1.7 copy.22

commit v2 on v0

v2 whole, which is shorter than its diff:
```python
import functools

import jax
import jax.numpy as jnp
from jax import lax
from jax.experimental import pallas as pl
from jax.experimental.pallas import tpu as pltpu
from jax.sharding import PartitionSpec as P

bf16, f32 = jnp.bfloat16, jnp.float32
MESH = pl.DeviceIdType.MESH
LINE = 4
NB = 512
SLOTS = 3
RB = 16
LN_ROWS = 64
VMEM_LIMIT = 66_500_000


CORE, Y, X, Y_CORE = (0, 0, 1), (0, 1, 0), (1, 0, 0), (0, 1, 1)


def shift(flips):
    data, sp = lax.axis_index("data"), lax.axis_index("sp")
    y, core = sp // 2, sp % 2
    return {"data": 1 - data if flips[0] else data, "sp": (1 - y if flips[1] else y) * 2 + (1 - core if flips[2] else core)}


def place_of(device):
    return device["data"] * 4 + device["sp"]


class Line:
    def __init__(self):
        self.z = lax.axis_index("tp")

    def exists(self, direction):
        return self.z < LINE - 1 if direction == 0 else self.z > 0

    def source_exists(self, direction):
        return self.z > 0 if direction == 0 else self.z < LINE - 1

    def target(self, direction):
        return {"tp": self.z + 1 if direction == 0 else self.z - 1}

    def origin(self, direction, hop):
        return self.z - hop if direction == 0 else self.z + hop

    def sends(self, direction, hop):
        o = self.origin(direction, hop)
        return jnp.logical_and(self.exists(direction), jnp.logical_and(o >= 0, o < LINE))

    def receives(self, direction, hop):
        o = self.origin(direction, hop + 1)
        return jnp.logical_and(o >= 0, o < LINE)


def remote(src, dst, send, recv, device):
    return pltpu.make_async_remote_copy(src_ref=src, dst_ref=dst, send_sem=send, recv_sem=recv, device_id=device, device_id_type=MESH)


class Gather:
    def __init__(self, line, own, slot, send, recv):
        self.line, self.own, self.slot, self.send, self.recv = line, own, slot, send, recv

    def copy(self, d, c, hop):
        o = jnp.clip(self.line.origin(d, hop), 0, LINE - 1)
        src = self.own(c) if hop == 0 else self.slot(c, o)
        return remote(src, self.slot(c, o), self.send.at[d, c, hop], self.recv.at[d, c, hop], self.line.target(d))

    def arrival(self, d, c, hop):
        o = jnp.clip(self.line.origin(d, hop + 1), 0, LINE - 1)
        here = self.slot(c, o)
        return remote(here, here, self.send.at[d, c, hop], self.recv.at[d, c, hop], self.line.target(d))

    def start(self, c, hop, only=lambda d: True):
        for d in range(2):
            @pl.when(jnp.logical_and(self.line.sends(d, hop), only(d)))
            def _():
                self.copy(d, c, hop).start()

    def arrive(self, c):
        for hop in range(LINE - 1):
            for d in range(2):
                self.settle(d, c, hop)

    def settle(self, d, c, hop):
        passed_on = self.line.sends(d, hop + 1) if hop + 1 < LINE - 1 else False

        @pl.when(jnp.logical_and(self.line.receives(d, hop), jnp.logical_not(passed_on)))
        def _():
            self.arrival(d, c, hop).wait_recv()

    def relay(self, c, hop, only=lambda d: True, wait=True):
        for d in range(2):
            @pl.when(jnp.logical_and(self.line.sends(d, hop), only(d)))
            def _():
                if wait:
                    self.arrival(d, c, hop - 1).wait_recv()
                self.copy(d, c, hop).start()

    def finish(self, chunks):
        for c in range(chunks):
            for hop in range(LINE - 1):
                for d in range(2):
                    @pl.when(self.line.sends(d, hop))
                    def _():
                        self.copy(d, c, hop).wait_send()


def meet(line, peers):
    barrier = pltpu.get_barrier_semaphore()
    for d in range(2):
        @pl.when(line.exists(d))
        def _():
            pl.semaphore_signal(barrier, inc=1, device_id=line.target(d), device_id_type=MESH)
    for p in peers:
        pl.semaphore_signal(barrier, inc=1, device_id=shift(p), device_id_type=MESH)
    pl.semaphore_wait(barrier, jnp.where(jnp.logical_or(line.z == 0, line.z == LINE - 1), 1, 2) + len(peers))


def normalize(src, dst, gain, bias, start, count):
    block = min(count, LN_ROWS)

    def some(i, _):
        at = pl.ds(pl.multiple_of(start + i * block, RB), block)
        u = src[at, :].astype(f32)
        u = u - jnp.mean(u, axis=-1, keepdims=True)
        var = jnp.mean(u * u, axis=-1, keepdims=True)
        dst[at, :] = (u * lax.rsqrt(var + 1e-6) * gain[...] + bias[...]).astype(bf16)
        return 0

    lax.fori_loop(0, count // block, some, 0)


class Phase:
    def __init__(self, count, copies, compute, after=None, middle=None):
        self.count, self.copies, self.compute, self.after, self.middle = count, copies, compute, after, middle

    def start(self, n, slot):
        for when, copy in self.copies(n, slot):
            when(copy.start) if when else copy.start()

    def wait(self, n, slot):
        for when, copy in self.copies(n, slot):
            when(copy.wait) if when else copy.wait()


def run_phases(phases, prepare):
    flat = [(p, n) for p in phases for n in range(p.count)]
    ahead = SLOTS - 1
    for i in range(ahead):
        flat[i][0].start(flat[i][1], i)
    prepare()
    base = 0
    for p in phases:
        later = flat[base + p.count : base + p.count + ahead]

        def step(n, _):
            slot = lax.rem(base + n, SLOTS)
            if p.count > ahead:
                @pl.when(n + ahead < p.count)
                def _():
                    p.start(n + ahead, lax.rem(base + n + ahead, SLOTS))
            for j, (q, m) in enumerate(later):
                when = p.count + j - ahead
                if when >= 0:
                    @pl.when(n == when)
                    def _():
                        q.start(m, (base + p.count + j) % SLOTS)
            p.wait(n, slot)
            p.compute(n, slot)
            if p.middle:
                pl.when(n == min(p.count // 2 + 1, p.count - 1))(p.middle)
            return 0

        if p.count == 1:
            step(0, 0)
        else:
            lax.fori_loop(0, p.count, step, 0)
        if p.after:
            p.after()
        base += p.count


class PlaneGather:
    def __init__(self, line, own, wg, ws, wr, ps, pr, fs, fr):
        width = wg.shape[2]
        cols = width // 8
        self.line, self.wg, self.ps, self.pr, self.fs, self.fr = line, wg, ps, pr, fs, fr
        self.cols = lambda p: pl.ds(pl.multiple_of(p * cols, 128), cols)
        me = shift((0, 0, 0))
        self.place = place_of(me)
        self.core = lax.axis_index("sp") % 2
        self.along = Gather(line, lambda c: own.at[:, self.cols(self.place)], lambda c, o: wg.at[o, :, self.cols(self.place)], ws, wr)
        across, beside = shift(X), shift(Y)
        first_is_x = self.core == 0
        self.diagonal_device = {k: jnp.where(first_is_x, beside[k], across[k]) for k in across}
        self.diagonal_given = jnp.where(first_is_x, place_of(across), place_of(beside))
        self.sources = (place_of(shift(CORE)), place_of(beside), place_of(across), place_of(shift((1, 1, 0))))

    def each(self, hop, action, only=lambda d: True):
        for d in range(2):
            @pl.when(jnp.logical_and(self.line.receives(d, hop), only(d)))
            def _():
                o = jnp.clip(self.line.origin(d, hop + 1), 0, LINE - 1)
                action(d, lambda p: self.wg.at[o, :, self.cols(p)])

    def direct(self, d, hop, k, ref):
        return remote(ref, ref, self.ps.at[d, hop, k], self.pr.at[d, hop, k], shift((CORE, Y, X)[k]))

    def diagonal(self, d, hop, ref):
        return remote(ref, ref, self.ps.at[d, hop, 3], self.pr.at[d, hop, 3], self.diagonal_device)

    def pass_on(self, d, hop, k, ref):
        return remote(ref, ref, self.fs.at[d, hop, k - 1], self.fr.at[d, hop, k - 1], shift(CORE))

    def spread(self, hop, only=lambda d: True, wait="unless relayed"):
        def action(d, slab):
            if wait == "always":
                self.along.arrival(d, 0, hop).wait_recv()
            elif wait == "unless relayed":
                self.along.settle(d, 0, hop)
            for k in range(3):
                self.direct(d, hop, k, slab(self.place)).start()

        self.each(hop, action, only)

    def forward(self, hop, only=lambda d: True):
        def action(d, slab):
            for k in (1, 2):
                self.direct(d, hop, k, slab(self.sources[k])).wait_recv()
                self.pass_on(d, hop, k, slab(self.sources[k])).start()
            self.diagonal(d, hop, slab(self.diagonal_given)).start()

        self.each(hop, action, only)

    def forward_diagonal(self, hop, only=lambda d: True):
        def action(d, slab):
            self.diagonal(d, hop, slab(self.sources[3])).wait_recv()
            self.pass_on(d, hop, 3, slab(self.sources[3])).start()

        self.each(hop, action, only)

    def arrive(self, hops):
        for hop in hops:
            def action(d, slab):
                self.direct(d, hop, 0, slab(self.sources[0])).wait_recv()
                for k in (1, 2, 3):
                    p = self.sources[k]
                    self.pass_on(d, hop, k, slab(p + 1 - 2 * (p % 2))).wait_recv()

            self.each(hop, action)

    def finish(self, hops):
        for hop in hops:
            def action(d, slab):
                for k in range(3):
                    self.direct(d, hop, k, slab(self.place)).wait_send()
                self.diagonal(d, hop, slab(self.diagonal_given)).wait_send()
                for k in (1, 2, 3):
                    self.pass_on(d, hop, k, slab(self.sources[k])).wait_send()

            self.each(hop, action)


def block_kernel(b, step, *refs):
    names = ["x", "gains", "biases", "wq", "wo", "wu", "wd"] + ([] if b == 0 else ["wg_in"])
    names += ["turned", "r", "og", "o", "part"] + (["wg0", "wg1"] if b == 0 else ["wg1"])
    names += ["rv", "nv", "qkv", "ov", "gv", "mine", "wbuf", "far_got", "got", "add", "pst"]
    names += ["xs", "xr", "os", "or_", "rs", "rr", "vs", "vr", "ls", "ts", "ds", "hs", "hr", "ws", "wr", "ps", "pr", "fs", "fr"]
    v = dict(zip(names, refs, strict=True))
    x, r, o, og, part, turned = (v[k] for k in ("x", "r", "o", "og", "part", "turned"))
    wq, wo, wu, wd = (v[k] for k in ("wq", "wo", "wu", "wd"))
    rv, nv, qkv, ov, gv, mine, wbuf, far_got, got, add, pst = (v[k] for k in ("rv", "nv", "qkv", "ov", "gv", "mine", "wbuf", "far_got", "got", "add", "pst"))
    rs, rr, vs, vr, ls, ts, ds = (v[k] for k in ("rs", "rr", "vs", "vr", "ls", "ts", "ds"))
    wg = v[f"wg{b}"]
    chunks, rows, width = x.shape
    tokens = rows * LINE
    hk, hidden = wo.shape[1], wu.shape[2]
    heads = hk // 128
    line = Line()
    z = line.z
    xg = Gather(line, lambda c: x.at[c], lambda c, s: r.at[c, s], v["xs"], v["xr"])
    og_ = Gather(line, lambda c: o.at[c], lambda c, s: og.at[c, s], v["os"], v["or_"])
    w0, w1 = (PlaneGather(line, wo.at[i], v[f"wg{i}"], *(v[k].at[i] for k in ("ws", "wr", "ps", "pr", "fs", "fr"))) if i >= b else None for i in range(2))

    def rows_of(o):
        return pl.ds(pl.multiple_of(o * rows, rows), rows)

    def columns(n):
        return pl.ds(pl.multiple_of(n * NB, 128), NB)

    def load_r(c):
        copies = []
        for s in range(LINE):
            there = rv.at[pl.ds(s * rows, rows), :]
            copies.append((z == s, pltpu.make_async_copy(x.at[c], there, ls.at[s]), pltpu.make_async_copy(r.at[c, s], there, ls.at[s])))
        for own, a, other in copies:
            pl.when(own)(a.start)
            pl.when(jnp.logical_not(own))(other.start)
        for _, a, _ in copies:
            a.wait()

    per_tile = NB // 128

    def qkv_phase(c, first, count, wide, middle=None):
        def copies(n, slot):
            return [(None, pltpu.make_async_copy(wq.at[b, (first + n) * per_tile + i], wbuf.at[slot, :, pl.ds(i * 128, 128)], ts.at[slot, i])) for i in range(wide)]

        def compute(n, slot):
            at = pl.ds(pl.multiple_of((first + n) * NB, 128), wide * 128)
            qkv[:, at] = jnp.dot(nv[...], wbuf[slot, :, : wide * 128], preferred_element_type=f32).astype(bf16)

        return Phase(count, copies, compute, None, middle)

    def queries(c, middle=None):
        full, rest = divmod(3 * heads, per_tile)
        phases = [qkv_phase(c, 0, full, per_tile, middle)] + ([qkv_phase(c, full, 1, rest)] if rest else [])

        def piece(o, sem, source):
            return pltpu.make_async_copy(source, rv.at[rows_of(o), :], sem)

        def prepare():
            own = piece(z, ls.at[0], x.at[c])
            own.start()
            before = [(None, own, z)]
            for hop in range(LINE):
                now = []
                if hop < LINE - 1:
                    for d in range(2):
                        origin = jnp.clip(line.origin(d, hop + 1), 0, LINE - 1)
                        now.append((line.receives(d, hop), piece(origin, ls.at[1 + d * (LINE - 1) + hop], r.at[c, origin]), origin))
                        xg.settle(d, c, hop)
                        pl.when(now[-1][0])(now[-1][1].start)
                for there, copy, origin in before:
                    def finish():
                        copy.wait()
                        normalize(rv, nv, v["gains"].at[b, pl.ds(0, 1)], v["biases"].at[b, pl.ds(0, 1)], origin * rows, rows)

                    finish() if there is None else pl.when(there)(finish)
                before = now

        run_phases(phases, prepare)

    def attend(c):
        if step:
            key = lambda t: t // rows * step + t % step
            mask = key(lax.broadcasted_iota(jnp.int32, (tokens, tokens), 0)) == key(lax.broadcasted_iota(jnp.int32, (tokens, tokens), 1))

        def head(h, _):
            at = lambda i: pl.ds(pl.multiple_of((i * heads + h) * 128, 128), 128)
            s = lax.dot_general(qkv[:, at(0)], qkv[:, at(1)], (((1,), (1,)), ((), ())), preferred_element_type=f32) * 128**-0.5
            if step:
                s = jnp.where(mask, s, -1e30)
            e = jnp.exp(s - jnp.max(s, axis=-1, keepdims=True))
            p = (e * (1.0 / jnp.sum(e, axis=-1, keepdims=True))).astype(bf16)
            ov[:, pl.ds(pl.multiple_of(h * 128, 128), 128)] = jnp.dot(p, qkv[:, at(2)], preferred_element_type=f32).astype(bf16)
            return 0

        lax.fori_loop(0, heads, head, 0)
        out = pltpu.make_async_copy(ov, o.at[c], ls.at[LINE])
        out.start()
        out.wait()

    def load_o(c):
        both = []
        for s in range(LINE):
            there = nv.at[:, pl.ds(s * hk, hk)]
            both.append((z == s, pltpu.make_async_copy(o.at[c], there, ls.at[s]), pltpu.make_async_copy(og.at[c, s], there, ls.at[s])))
        for own, a, other in both:
            pl.when(own)(a.start)
            pl.when(jnp.logical_not(own))(other.start)
        for _, a, _ in both:
            a.wait()

    def out_phase(c, after, middle):
        def copies(n, slot):
            result = []
            for s in range(LINE):
                there = wbuf.at[slot, pl.ds(s * hk, hk), :]
                result.append((pl.when(z == s), pltpu.make_async_copy(wo.at[b, :, columns(n)], there, ts.at[slot, s])))
                result.append((pl.when(z != s), pltpu.make_async_copy(wg.at[s, :, columns(n)], there, ts.at[slot, s])))
            return result

        def compute(n, slot):
            a = jnp.dot(nv[...], wbuf[slot], preferred_element_type=f32).astype(bf16)
            rv[:, columns(n)] = (rv[:, columns(n)].astype(f32) + a.astype(f32)).astype(bf16)

        return Phase(width // NB, copies, compute, after, middle)

    def up_phase(first, count, wide, after=None):
        cols = lambda n: pl.ds(pl.multiple_of((first + n) * NB, 128), wide)

        def copies(n, slot):
            return [(None, pltpu.make_async_copy(wu.at[b, :, cols(n)], wbuf.at[slot, :, pl.ds(0, wide)], ts.at[slot, 0]))]

        def compute(n, slot):
            u = jnp.dot(nv[...], wbuf[slot, :, :wide], preferred_element_type=f32).astype(bf16).astype(f32)
            gv[:, cols(n)] = jax.nn.gelu(u, approximate=True).astype(bf16)

        return Phase(count, copies, compute, after)

    def down_phase(c, middle):
        count = width // NB

        def store(n, slot):
            return pltpu.make_async_copy(pst.at[slot], part.at[c, :, columns(n)], ds.at[slot])

        def copies(n, slot):
            return [(None, pltpu.make_async_copy(wd.at[b, :, columns(n)], wbuf.at[slot, pl.ds(0, hidden), :], ts.at[slot, 0]))]

        def compute(n, slot):
            s = lax.rem(n, 2)

            @pl.when(n >= 2)
            def _():
                store(n - 2, s).wait()

            pst[s] = jnp.dot(gv[...], wbuf[slot, :hidden, :], preferred_element_type=f32)
            store(n, s).start()

        def after():
            for n in range(max(count - 2, 0), count):
                store(n, n % 2).wait()

        return Phase(count, copies, compute, after, middle)

    def feed(c, mid_out=None, after_out=None, after_up=None, mid_down=None):
        full, rest = divmod(hidden, NB)

        def prepare():
            load_r(c)
            load_o(c)

        def out_done():
            normalize(rv, nv, v["gains"].at[b, pl.ds(1, 1)], v["biases"].at[b, pl.ds(1, 1)], 0, tokens)
            mine[c] = rv[rows_of(z), :]
            if after_out:
                after_out()

        phases = [out_phase(c, out_done, mid_out), up_phase(0, full, NB, None if rest else after_up)]
        if rest:
            phases.append(up_phase(full, 1, rest, after_up))
        run_phases(phases + [down_phase(c, mid_down)], prepare)

    def term(c, t):
        return part.at[c, rows_of(t), :]

    def slot_of(d, c, far):
        return far_got.at[c] if far == LINE - 1 else got.at[d, c, LINE - 2 - far]

    def hop_copy(d, c, far, src):
        return remote(src, slot_of(d, c, far), rs.at[d, c, LINE - 1 - far], rr.at[d, c, LINE - 1 - far], line.target(d))

    def first(d):
        return z == 0 if d == 0 else z == LINE - 1

    def far_target(d, far):
        return z + far if d == 0 else z - far

    half = width // 2
    early = width // NB // 2 + 1 < width // NB

    def early_copy(d):
        cols = pl.ds(0, half)
        src = part.at[0, rows_of(LINE - 1 if d == 0 else 0), cols]
        return remote(src, far_got.at[0, :, cols], v["hs"].at[d], v["hr"].at[d], line.target(d))

    def rest_copy(d):
        cols = pl.ds(half, half)
        src = part.at[0, rows_of(LINE - 1 if d == 0 else 0), cols]
        return remote(src, far_got.at[0, :, cols], rs.at[d, 0, 0], rr.at[d, 0, 0], line.target(d))

    def split(c, far):
        return early and c == 0 and far == LINE - 1

    def reduce_early():
        for d in range(2):
            pl.when(first(d))(lambda: early_copy(d).start())

    def reduce_start(c, fars):
        for far in fars:
            for d in range(2):
                @pl.when(first(d))
                def _():
                    copy = rest_copy(d) if split(c, far) else hop_copy(d, c, far, term(c, far if d == 0 else LINE - 1 - far))
                    copy.start()

    def middle(d, far):
        t = far_target(d, far - 1)
        return jnp.logical_and(jnp.logical_not(first(d)), jnp.logical_and(t >= 0, t < LINE))

    def reduce_relay(c, far):
        for d in range(2):
            @pl.when(middle(d, far))
            def _():
                t = jnp.clip(far_target(d, far - 1), 0, LINE - 1)
                fetch = pltpu.make_async_copy(term(c, t), add, ls.at[LINE + 1])
                fetch.start()
                slot = slot_of(d, c, far)
                if split(c, far):
                    early_copy(d).wait_recv()
                    rest_copy(d).wait_recv()
                else:
                    hop_copy(d, c, far, slot).wait_recv()
                fetch.wait()

                def some(i, _):
                    at = pl.ds(pl.multiple_of(i * RB, RB), RB)
                    slot[at, :] = slot[at, :] + add[at, :]
                    return 0

                lax.fori_loop(0, rows // RB, some, 0)
                hop_copy(d, c, far - 1, slot).start()

    part_rows = rows // 4
    sp = lax.axis_index("sp")

    def turn(c, k):
        device = shift((CORE, Y, Y_CORE)[k])
        there = mine.at[c, pl.ds(pl.multiple_of(device["sp"] * part_rows, part_rows), part_rows), :]
        return remote(there, turned.at[sp * 4 + c], vs.at[c, k], vr.at[c, k], device)

    def turn_own(c):
        return pltpu.make_async_copy(mine.at[c, pl.ds(pl.multiple_of(sp * part_rows, part_rows), part_rows), :], turned.at[sp * 4 + c], ds.at[2 + c])

    def turn_arrive(c, k):
        device = shift((CORE, Y, Y_CORE)[k])
        here = turned.at[device["sp"] * 4 + c]
        remote(here, here, vs.at[c, k], vr.at[c, k], device).wait_recv()

    def reduce_finish(c):
        fetch = pltpu.make_async_copy(term(c, z), add, ls.at[LINE + 1])
        fetch.start()
        for d in range(2):
            @pl.when(jnp.logical_not(first(d)))
            def _():
                hop_copy(d, c, 1, slot_of(d, c, 1)).wait_recv()
        fetch.wait()

        def some(i, _):
            at = pl.ds(pl.multiple_of(i * RB, RB), RB)
            for d in range(2):
                @pl.when(jnp.logical_not(first(d)))
                def _():
                    add[at, :] = add[at, :] + got[d, c, LINE - 3, at, :]
            m = add[at, :].astype(bf16)
            mine[c, at, :] = (mine[c, at, :].astype(f32) + m.astype(f32)).astype(bf16)
            return 0

        lax.fori_loop(0, rows // RB, some, 0)
        turn_own(c).start()
        for k in range(3):
            turn(c, k).start()

    def reduce_sent(c):
        for far in range(LINE - 1, 0, -1):
            for d in range(2):
                @pl.when(first(d))
                def _():
                    if split(c, far):
                        early_copy(d).wait_send()
                        rest_copy(d).wait_send()
                    else:
                        hop_copy(d, c, far, term(c, 0)).wait_send()
                if far > 1:
                    @pl.when(middle(d, far))
                    def _():
                        hop_copy(d, c, far - 1, slot_of(d, c, far)).wait_send()

    outward = lambda d: z == (LINE - 2 if d == 0 else 1)
    inward = lambda d: jnp.logical_not(outward(d))
    inner = lambda d: jnp.logical_and(z > 0, z < LINE - 1)
    outer = lambda d: jnp.logical_not(inner(d))
    both = lambda p, q: (lambda d: jnp.logical_and(p(d), q(d)))

    def later(function):
        return lambda *args, **hooks: functools.partial(function, *args, **hooks)

    def hook(*actions):
        def run():
            for action in actions:
                action()

        return run

    c0, c1, c2, c3 = h0, h1, h2, h3 = range(LINE)
    outwards = (h3, h2, h1)
    XS, XR, OS, OR, OA = later(xg.start), later(xg.relay), later(og_.start), later(og_.relay), later(og_.arrive)
    Q, A, B = later(queries), later(attend), later(feed)
    RS, RR, F = later(reduce_start), later(reduce_relay), later(reduce_finish)
    early_half = reduce_early if early else hook()
    VS, VR = later(w1.along.start), later(w1.along.relay)
    VP, VF, VD = later(w1.spread), later(w1.forward), later(w1.forward_diagonal)

    if b == 0:
        US, UR, UP, UF, UD = (later(f) for f in (w0.along.start, w0.along.relay, w0.spread, w0.forward, w0.forward_diagonal))
        lead = [US(c0, h0), UR(c0, h1), UP(h0), UR(c0, h2), XS(c0, h0), VS(c0, h0, first), XR(c0, h1), VS(c0, h0, both(inner, inward))]
        lead += [UP(h1), UF(h0), UP(h2), XR(c0, h2), XS(c1, h0), XR(c1, h1)]
        after_a0, after_q1, after_a1 = [UD(h0), UF(h1), UF(h2)], [UD(h1)], [UD(h2), later(w0.arrive)(range(h3))]
        after_b0, after_b1, after_rr13 = [VP(h0, inner, "always")], [VF(h0, inner)], [VD(h0, inner)]
        in_b2, after_b2 = [VS(c0, h0, both(inner, outward)), VR(c0, h1, outward, False)], [VR(c0, h1, inward, False)]
        tail0 = [VP(h1, inner, "always"), VP(h0, outer)]
        tail1 = [VR(c0, h2, wait=False), VF(h0, outer), VP(h1, outer)]
        tail2 = [VF(h1, inner)]
        tail3 = [VD(h0, outer), VD(h1, inner), VF(h1, outer)]
        last = [VD(h1, outer), later(w1.arrive)(range(h2))] + [later(w1.along.settle)(d, c0, h2) for d in range(h2)]
        last += [later(w0.along.finish)(h1), later(w0.finish)(range(h3)), later(w1.along.finish)(h1), later(w1.finish)(range(h2))]
    else:
        lead = [VP(h2, wait="never"), XS(c0, h0), XR(c0, h1), XR(c0, h2), XS(c1, h0), XR(c1, h1)]
        after_a0, after_q1, after_a1, last = [VF(h2)], [VD(h2)], [later(w1.arrive)((h2,))], [later(w1.finish)((h2,))]
        after_b0 = after_b1 = after_rr13 = in_b2 = after_b2 = tail0 = tail1 = tail2 = tail3 = []
    schedule = lead + [Q(c0, middle=XR(c1, h2)), A(c0), OS(c0, h0)] + after_a0 + [OR(c0, h1), Q(c1, middle=OR(c0, h2)), XS(c2, h0)] + after_q1
    schedule += [A(c1)] + after_a1 + [OA(c0)]
    schedule += [B(c0, mid_out=XR(c2, h1), after_out=XR(c2, h2), after_up=hook(OS(c1, h0), XS(c3, h0)), mid_down=early_half), RS(c0, outwards), OR(c1, h1)]
    schedule += after_b0 + [Q(c2, middle=hook(OR(c1, h2), XR(c3, h1))), A(c2), OA(c1)]
    schedule += [B(c1, mid_out=RR(c0, h3), after_out=XR(c3, h2), after_up=hook(OS(c2, h0), RR(c0, h2))), RS(c1, outwards[:1])] + after_b1
    schedule += [Q(c3, middle=hook(OR(c2, h1), F(c0))), OR(c2, h2), A(c3), OS(c3, h0), RS(c1, outwards[1:]), RR(c1, h3)] + after_rr13 + [OA(c2)]
    schedule += [B(c2, mid_out=OR(c3, h1), after_out=OR(c3, h2), after_up=hook(RR(c1, h2), *in_b2)), RS(c2, outwards)] + after_b2 + [OA(c3)]
    schedule += [B(c3, after_out=F(c1), after_up=RR(c2, h3)), RS(c3, outwards)] + tail0 + [RR(c2, h2)] + tail1 + [F(c2)] + tail2
    schedule += [RR(c3, h3)] + tail3 + [RR(c3, h2), F(c3)] + last
    meet(line, (CORE, Y, X, Y_CORE))
    for action in schedule:
        action()
    xg.finish(chunks)
    og_.finish(chunks)
    for c in range(chunks):
        reduce_sent(c)
        turn_own(c).wait()
        for k in range(3):
            turn(c, k).wait_send()
            turn_arrive(c, k)


ANY = pl.BlockSpec(memory_space=pl.ANY)
VMEM = pl.BlockSpec(memory_space=pltpu.VMEM)
DMA = pltpu.SemaphoreType.DMA


def call_block(b, step, x, gains, biases, wq, wo, wu, wd, wg):
    chunks, rows, width = x.shape
    hk, tokens, hidden = wo.shape[1], rows * LINE, wu.shape[2]
    hops = LINE - 1
    shape = jax.ShapeDtypeStruct
    outs = [shape((4 * chunks, rows // 4, width), bf16), shape((chunks, LINE, rows, width), bf16), shape((chunks, LINE, tokens, hk), bf16)]
    outs += [shape((chunks, tokens, hk), bf16), shape((chunks, tokens, width), f32)]
    line_sems = DMA((2, chunks, hops))
    scratch = [
        pltpu.VMEM((tokens, width), bf16), pltpu.VMEM((tokens, width), bf16), pltpu.VMEM((tokens, 3 * hk), bf16), pltpu.VMEM((tokens, hk), bf16),
        pltpu.VMEM((tokens, hidden), bf16), pltpu.VMEM((chunks, rows, width), bf16), pltpu.VMEM((SLOTS, width, NB), bf16),
        pltpu.VMEM((chunks, rows, width), f32), pltpu.VMEM((2, chunks, 2, rows, width), f32), pltpu.VMEM((rows, width), f32), pltpu.VMEM((2, tokens, NB), f32),
        line_sems, line_sems, line_sems, line_sems, line_sems, line_sems, DMA((chunks, 3)), DMA((chunks, 3)), DMA((2 * LINE,)), DMA((SLOTS, LINE)), DMA((2 + chunks,)), DMA((2,)), DMA((2,)),
    ]
    outs += [shape((LINE, hk, width), bf16)] * (2 - b)
    scratch += [DMA((2, 2, 1, hops)), DMA((2, 2, 1, hops)), DMA((2, 2, hops, 4)), DMA((2, 2, hops, 4)), DMA((2, 2, hops, 3)), DMA((2, 2, hops, 3))]
    args = [x, gains, biases, wq, wo, wu, wd] + ([] if b == 0 else [wg])
    results = pl.pallas_call(
        functools.partial(block_kernel, b, step),
        out_shape=tuple(outs),
        in_specs=[ANY, VMEM, VMEM] + [ANY] * (len(args) - 3),
        out_specs=tuple(ANY for _ in outs),
        scratch_shapes=scratch,
        input_output_aliases={} if b == 0 else {len(args) - 1: len(outs) - 1},
        compiler_params=pltpu.CompilerParams(collective_id=b, has_side_effects=True, vmem_limit_bytes=VMEM_LIMIT),
        name=f"block_{b}",
    )(*args)
    return results[0], results[-1]


def reorder(a, sizes, order):
    n = a.shape[0] * a.shape[1]
    source = jnp.arange(n).reshape(sizes).transpose(order).reshape(n, 1)
    one_hot = (source == jnp.arange(n)[None]).astype(a.dtype)
    return jnp.dot(one_hot, a.reshape(n, -1), preferred_element_type=f32).astype(a.dtype)


def solution(mesh):
    act_spec = P("data", "sp", "tp", None)
    weight_specs = (P(), P(), P(None, None, None, "tp", None), P(None, "tp", None, None), P(None, None, "tp"), P(None, "tp", None))

    def device_program(x, ln_gain, ln_bias, w_qkv, w_out, w_up, w_down):
        _, frames, rows, width = x.shape
        wq = w_qkv.transpose(0, 2, 3, 1, 4).reshape(2, -1, width, 128)
        wo = w_out.reshape(2, -1, width)
        per = rows // 4
        step = per // 4

        def block(b, r, wg):
            return call_block(b, step if b else 0, r, ln_gain, ln_bias, wq, wo, w_up, w_down, wg)

        spatial, wg = block(0, x[0], None)
        turned = reorder(spatial, (4 * frames, 4, step), (1, 0, 2)).reshape(4, -1, width)
        temporal, _ = block(1, turned, wg)
        return reorder(temporal, (4, 4, frames, step), (2, 0, 1, 3)).reshape(1, frames, rows, width)

    return jax.shard_map(device_program, mesh=mesh, in_specs=(act_spec,) + weight_specs, out_specs=act_spec, check_vma=False)
```

time: 2640 us -> 1280 us (0.48)
  waiting for transfers between devices: 2120 us -> 0 us
  Pallas kernels: 0 us -> 1270 us
  matrix products: 364 us -> 8.26 us
  blocking collectives: 68.2 us -> 0 us
  other arithmetic: 61.6 us -> 0.02 us
    reduce_scatter x4 -> x0, waiting for transfers between devices: 1380 us -> none  [the longest x2 688 us: local_block(): lax.psum_scatter(part_sum, 'tp', scatter_dimension=2, tiled=True)]
    pallas_call x0 -> x2, Pallas kernels: none -> 1270 us  [call_block(): pl.pallas_call(functools.partial(block_kernel, b, step), out_shape=tuple(...]
    all_gather x4 -> x0, waiting for transfers between devices: 743 us -> none  [the longest x2 372 us: local_block(): lax.all_gather(layer_norm(hidden, gain[1], shift[1]), 'tp', axis=2, tiled...]
    dot_general x11 -> x2, matrix products: 364 us -> 8.26 us  [reorder(): jnp.dot(one_hot, a.reshape(n, -1), preferred_element_type=f32)]
    all_to_all x2 -> x0, blocking collectives: 68.2 us -> none  [the longest x1 34.1 us: device_program(): return lax.all_to_all(temporal, 'sp', 1, 2, tiled=True)]
  transfers between devices with their start and end apart: 8 -> 0, of which waited for: 8 -> 0; matrix products, arithmetic and copies ran while one was open for 0% -> 0% of each run, Pallas kernels for 0% -> 0%
where the time goes in v2:
time: 1280 us; the launch traced here: 1270 us
  Pallas kernels  1270 us (99%)
    pallas_call x2, Pallas kernels, call_block(): pl.pallas_call(functools.partial(block_kernel, b, step), out_shape=tuple(...  1270 us

profile of v2, /device:TPU:1, one launch (start us, length us, event | category | flops | bytes accessed | tf_op | source)
XLA Modules:
  0.0 1274.6 jit_solution(9650530324237598439)
XLA Ops:
  0.0 687.3 %block_0.1 = (bf16[16,16,5120]{2,1,0:T(8,128)(2,1)}, bf16[4,4,64,5120]{3,2,1,0:T(8,128)(2,1)}, bf16[4,4,256,1280]{3,2,1,0:T(8,128)(2,1)}, bf16[4,256,1280]{2,1,0...) custom-call(bf16[4,64,5120]{2,1,0:T(8,128)(2,1)} %bitcast.16, ...), custom_call_target="tpu_custom_call" | custom-call | tf_op jit(solution)/shard_map/block_0/pallas_call | solution.py:658
  687.3 0.1 reshape.139
  687.4 4.1 convolution_convert_fusion.1
  691.6 578.3 %block_1.1 = (bf16[16,16,5120]{2,1,0:T(8,128)(2,1)}, bf16[4,4,64,5120]{3,2,1,0:T(8,128)(2,1)}, bf16[4,4,256,1280]{3,2,1,0:T(8,128)(2,1)}, bf16[4,256,1280]{2,1,0...) custom-call(bf16[4,64,5120]{2,1,0:T(8,128)(2,1)} %bitcast.13, ...), custom_call_target="tpu_custom_call", output_to_operand_aliasing={{5}: (7, {})} | custom-call | tf_op jit(solution)/shard_map/block_1/pallas_call | solution.py:658
  1269.9 0.1 reshape.132
  1270.0 4.1 convolution_convert_fusion
  (2 shorter events, 0.0 us)

commit v3 on v2

--- a/solution.py
+++ b/solution.py
@@ -28,6 +28,9 @@
 
 def place_of(device):
     return device["data"] * 4 + device["sp"]
+
+
+ARRIVALS = (((1, 0), (0, 0), (0, 0), (0, 0)), ((1, 1), (1, 0), (1, 0), (0, 1)), ((1, 2), (1, 1), (0, 1), (0, 2)))
 
 
 class Line:
@@ -134,8 +137,8 @@
 
 
 class Phase:
-    def __init__(self, count, copies, compute, after=None, middle=None):
-        self.count, self.copies, self.compute, self.after, self.middle = count, copies, compute, after, middle
+    def __init__(self, count, copies, compute, after=None, middle=None, before=None):
+        self.count, self.copies, self.compute, self.after, self.middle, self.before = count, copies, compute, after, middle, before
 
     def start(self, n, slot):
         for when, copy in self.copies(n, slot):
@@ -174,6 +177,8 @@
                 pl.when(n == min(p.count // 2 + 1, p.count - 1))(p.middle)
             return 0
 
+        if p.before:
+            p.before()
         if p.count == 1:
             step(0, 0)
         else:
@@ -267,12 +272,13 @@
 def block_kernel(b, step, *refs):
     names = ["x", "gains", "biases", "wq", "wo", "wu", "wd"] + ([] if b == 0 else ["wg_in"])
     names += ["turned", "r", "og", "o", "part"] + (["wg0", "wg1"] if b == 0 else ["wg1"])
-    names += ["rv", "nv", "qkv", "ov", "gv", "mine", "wbuf", "far_got", "got", "add", "pst"]
+    scratch_names = ["rv", "nv", "qkv", "ov", "gv", "mine", "acc", "wbuf", "far_got", "got", "add", "pst"]
+    names += scratch_names
     names += ["xs", "xr", "os", "or_", "rs", "rr", "vs", "vr", "ls", "ts", "ds", "hs", "hr", "ws", "wr", "ps", "pr", "fs", "fr"]
     v = dict(zip(names, refs, strict=True))
     x, r, o, og, part, turned = (v[k] for k in ("x", "r", "o", "og", "part", "turned"))
     wq, wo, wu, wd = (v[k] for k in ("wq", "wo", "wu", "wd"))
-    rv, nv, qkv, ov, gv, mine, wbuf, far_got, got, add, pst = (v[k] for k in ("rv", "nv", "qkv", "ov", "gv", "mine", "wbuf", "far_got", "got", "add", "pst"))
+    rv, nv, qkv, ov, gv, mine, acc, wbuf, far_got, got, add, pst = (v[k] for k in scratch_names)
     rs, rr, vs, vr, ls, ts, ds = (v[k] for k in ("rs", "rr", "vs", "vr", "ls", "ts", "ds"))
     wg = v[f"wg{b}"]
     chunks, rows, width = x.shape
@@ -291,16 +297,13 @@
     def columns(n):
         return pl.ds(pl.multiple_of(n * NB, 128), NB)
 
+    def r_copies(c, own=True):
+        return [pltpu.make_async_copy(x.at[c] if own else r.at[c, s], rv.at[rows_of(s), :], ls.at[s]) for s in range(LINE)]
+
     def load_r(c):
-        copies = []
-        for s in range(LINE):
-            there = rv.at[pl.ds(s * rows, rows), :]
-            copies.append((z == s, pltpu.make_async_copy(x.at[c], there, ls.at[s]), pltpu.make_async_copy(r.at[c, s], there, ls.at[s])))
-        for own, a, other in copies:
-            pl.when(own)(a.start)
-            pl.when(jnp.logical_not(own))(other.start)
-        for _, a, _ in copies:
-            a.wait()
+        for s, (a, other) in enumerate(zip(r_copies(c), r_copies(c, False))):
+            pl.when(z == s)(a.start)
+            pl.when(z != s)(other.start)
 
     per_tile = NB // 128
 
@@ -359,47 +362,61 @@
             return 0
 
         lax.fori_loop(0, heads, head, 0)
-        out = pltpu.make_async_copy(ov, o.at[c], ls.at[LINE])
+        out = pltpu.make_async_copy(ov, o.at[c], ls.at[2 * LINE])
         out.start()
         out.wait()
 
-    def load_o(c):
-        both = []
-        for s in range(LINE):
-            there = nv.at[:, pl.ds(s * hk, hk)]
-            both.append((z == s, pltpu.make_async_copy(o.at[c], there, ls.at[s]), pltpu.make_async_copy(og.at[c, s], there, ls.at[s])))
-        for own, a, other in both:
-            pl.when(own)(a.start)
-            pl.when(jnp.logical_not(own))(other.start)
-        for _, a, _ in both:
-            a.wait()
-
-    def out_phase(c, after, middle):
+    def block_of(i):
+        origins = [zz + (hop + 1 if d else -hop - 1) for zz, (d, hop) in enumerate(ARRIVALS[i - 1])]
+        return functools.reduce(lambda rest, zz: jnp.where(z == zz, origins[zz], rest), range(LINE), 0)
+
+    def fetch_o(c, i):
+        source = o.at[c] if i == 0 else og.at[c, block_of(i)]
+        return pltpu.make_async_copy(source, nv.at[:, pl.ds(i * hk, hk)], ls.at[LINE + i])
+
+    def arrive_o(c, i):
+        for zz, (d, hop) in enumerate(ARRIVALS[i - 1]):
+            pl.when(z == zz)(functools.partial(og_.settle, d, c, hop))
+        fetch_o(c, i).start()
+
+    def out_phase(c, i, after):
+        wide = 2 if width % (2 * NB) == 0 else 1
+
         def copies(n, slot):
-            result = []
-            for s in range(LINE):
-                there = wbuf.at[slot, pl.ds(s * hk, hk), :]
-                result.append((pl.when(z == s), pltpu.make_async_copy(wo.at[b, :, columns(n)], there, ts.at[slot, s])))
-                result.append((pl.when(z != s), pltpu.make_async_copy(wg.at[s, :, columns(n)], there, ts.at[slot, s])))
-            return result
+            source = wo.at[b] if i == 0 else wg.at[block_of(i)]
+            return [(None, pltpu.make_async_copy(source.at[:, columns(wide * n + j)], wbuf.at[slot, pl.ds(j * hk, hk), :], ts.at[slot, j])) for j in range(wide)]
 
         def compute(n, slot):
-            a = jnp.dot(nv[...], wbuf[slot], preferred_element_type=f32).astype(bf16)
-            rv[:, columns(n)] = (rv[:, columns(n)].astype(f32) + a.astype(f32)).astype(bf16)
-
-        return Phase(width // NB, copies, compute, after, middle)
-
-    def up_phase(first, count, wide, after=None):
-        cols = lambda n: pl.ds(pl.multiple_of((first + n) * NB, 128), wide)
+            for j in range(wide):
+                at = columns(wide * n + j)
+                a = jnp.dot(nv[:, i * hk : (i + 1) * hk], wbuf[slot, j * hk : (j + 1) * hk, :], preferred_element_type=f32)
+                if i > 0:
+                    a = acc[:, at] + a
+                if i < LINE - 1:
+                    acc[:, at] = a
+                else:
+                    rv[:, at] = (rv[:, at].astype(f32) + a.astype(bf16).astype(f32)).astype(bf16)
+
+        def before():
+            fetch_o(c, i).wait()
+            if i == LINE - 1:
+                for copy in r_copies(c):
+                    copy.wait()
+
+        middle = functools.partial(arrive_o, c, i + 1) if i < LINE - 1 else None
+        return Phase(width // (wide * NB), copies, compute, after, middle, before)
+
+    def up_phase(after):
+        cols = lambda n: pl.ds(pl.multiple_of(jnp.minimum(n * NB, hidden - NB), 128), NB)
 
         def copies(n, slot):
-            return [(None, pltpu.make_async_copy(wu.at[b, :, cols(n)], wbuf.at[slot, :, pl.ds(0, wide)], ts.at[slot, 0]))]
+            return [(None, pltpu.make_async_copy(wu.at[b, :, cols(n)], wbuf.at[slot], ts.at[slot, 0]))]
 
         def compute(n, slot):
-            u = jnp.dot(nv[...], wbuf[slot, :, :wide], preferred_element_type=f32).astype(bf16).astype(f32)
+            u = jnp.dot(nv[...], wbuf[slot], preferred_element_type=f32).astype(bf16).astype(f32)
             gv[:, cols(n)] = jax.nn.gelu(u, approximate=True).astype(bf16)
 
-        return Phase(count, copies, compute, after)
+        return Phase(pl.cdiv(hidden, NB), copies, compute, after)
 
     def down_phase(c, middle):
         count = width // NB
@@ -427,11 +444,9 @@
         return Phase(count, copies, compute, after, middle)
 
     def feed(c, mid_out=None, after_out=None, after_up=None, mid_down=None):
-        full, rest = divmod(hidden, NB)
-
         def prepare():
             load_r(c)
-            load_o(c)
+            fetch_o(c, 0).start()
 
         def out_done():
             normalize(rv, nv, v["gains"].at[b, pl.ds(1, 1)], v["biases"].at[b, pl.ds(1, 1)], 0, tokens)
@@ -439,9 +454,7 @@
             if after_out:
                 after_out()
 
-        phases = [out_phase(c, out_done, mid_out), up_phase(0, full, NB, None if rest else after_up)]
-        if rest:
-            phases.append(up_phase(full, 1, rest, after_up))
+        phases = [out_phase(c, i, after) for i, after in enumerate((None, mid_out, None, out_done))] + [up_phase(after_up)]
         run_phases(phases + [down_phase(c, mid_down)], prepare)
 
     def term(c, t):
@@ -496,7 +509,7 @@
             @pl.when(middle(d, far))
             def _():
                 t = jnp.clip(far_target(d, far - 1), 0, LINE - 1)
-                fetch = pltpu.make_async_copy(term(c, t), add, ls.at[LINE + 1])
+                fetch = pltpu.make_async_copy(term(c, t), add, ls.at[2 * LINE])
                 fetch.start()
                 slot = slot_of(d, c, far)
                 if split(c, far):
@@ -531,7 +544,7 @@
         remote(here, here, vs.at[c, k], vr.at[c, k], device).wait_recv()
 
     def reduce_finish(c):
-        fetch = pltpu.make_async_copy(term(c, z), add, ls.at[LINE + 1])
+        fetch = pltpu.make_async_copy(term(c, z), add, ls.at[2 * LINE])
         fetch.start()
         for d in range(2):
             @pl.when(jnp.logical_not(first(d)))
@@ -587,7 +600,7 @@
 
     c0, c1, c2, c3 = h0, h1, h2, h3 = range(LINE)
     outwards = (h3, h2, h1)
-    XS, XR, OS, OR, OA = later(xg.start), later(xg.relay), later(og_.start), later(og_.relay), later(og_.arrive)
+    XS, XR, OS, OR = later(xg.start), later(xg.relay), later(og_.start), later(og_.relay)
     Q, A, B = later(queries), later(attend), later(feed)
     RS, RR, F = later(reduce_start), later(reduce_relay), later(reduce_finish)
     early_half = reduce_early if early else hook()
@@ -612,12 +625,12 @@
         after_a0, after_q1, after_a1, last = [VF(h2)], [VD(h2)], [later(w1.arrive)((h2,))], [later(w1.finish)((h2,))]
         after_b0 = after_b1 = after_rr13 = in_b2 = after_b2 = tail0 = tail1 = tail2 = tail3 = []
     schedule = lead + [Q(c0, middle=XR(c1, h2)), A(c0), OS(c0, h0)] + after_a0 + [OR(c0, h1), Q(c1, middle=OR(c0, h2)), XS(c2, h0)] + after_q1
-    schedule += [A(c1)] + after_a1 + [OA(c0)]
+    schedule += [A(c1)] + after_a1
     schedule += [B(c0, mid_out=XR(c2, h1), after_out=XR(c2, h2), after_up=hook(OS(c1, h0), XS(c3, h0)), mid_down=early_half), RS(c0, outwards), OR(c1, h1)]
-    schedule += after_b0 + [Q(c2, middle=hook(OR(c1, h2), XR(c3, h1))), A(c2), OA(c1)]
+    schedule += after_b0 + [Q(c2, middle=hook(OR(c1, h2), XR(c3, h1))), A(c2)]
     schedule += [B(c1, mid_out=RR(c0, h3), after_out=XR(c3, h2), after_up=hook(OS(c2, h0), RR(c0, h2))), RS(c1, outwards[:1])] + after_b1
-    schedule += [Q(c3, middle=hook(OR(c2, h1), F(c0))), OR(c2, h2), A(c3), OS(c3, h0), RS(c1, outwards[1:]), RR(c1, h3)] + after_rr13 + [OA(c2)]
-    schedule += [B(c2, mid_out=OR(c3, h1), after_out=OR(c3, h2), after_up=hook(RR(c1, h2), *in_b2)), RS(c2, outwards)] + after_b2 + [OA(c3)]
+    schedule += [Q(c3, middle=hook(OR(c2, h1), F(c0))), OR(c2, h2), A(c3), OS(c3, h0), RS(c1, outwards[1:]), RR(c1, h3)] + after_rr13
+    schedule += [B(c2, mid_out=OR(c3, h1), after_out=OR(c3, h2), after_up=hook(RR(c1, h2), *in_b2)), RS(c2, outwards)] + after_b2
     schedule += [B(c3, after_out=F(c1), after_up=RR(c2, h3)), RS(c3, outwards)] + tail0 + [RR(c2, h2)] + tail1 + [F(c2)] + tail2
     schedule += [RR(c3, h3)] + tail3 + [RR(c3, h2), F(c3)] + last
     meet(line, (CORE, Y, X, Y_CORE))
@@ -648,9 +661,9 @@
     line_sems = DMA((2, chunks, hops))
     scratch = [
         pltpu.VMEM((tokens, width), bf16), pltpu.VMEM((tokens, width), bf16), pltpu.VMEM((tokens, 3 * hk), bf16), pltpu.VMEM((tokens, hk), bf16),
-        pltpu.VMEM((tokens, hidden), bf16), pltpu.VMEM((chunks, rows, width), bf16), pltpu.VMEM((SLOTS, width, NB), bf16),
+        pltpu.VMEM((tokens, hidden), bf16), pltpu.VMEM((chunks, rows, width), bf16), pltpu.VMEM((tokens, width), f32), pltpu.VMEM((SLOTS, width, NB), bf16),
         pltpu.VMEM((chunks, rows, width), f32), pltpu.VMEM((2, chunks, 2, rows, width), f32), pltpu.VMEM((rows, width), f32), pltpu.VMEM((2, tokens, NB), f32),
-        line_sems, line_sems, line_sems, line_sems, line_sems, line_sems, DMA((chunks, 3)), DMA((chunks, 3)), DMA((2 * LINE,)), DMA((SLOTS, LINE)), DMA((2 + chunks,)), DMA((2,)), DMA((2,)),
+        line_sems, line_sems, line_sems, line_sems, line_sems, line_sems, DMA((chunks, 3)), DMA((chunks, 3)), DMA((3 * LINE,)), DMA((SLOTS, LINE)), DMA((2 + chunks,)), DMA((2,)), DMA((2,)),
     ]
     outs += [shape((LINE, hk, width), bf16)] * (2 - b)
     scratch += [DMA((2, 2, 1, hops)), DMA((2, 2, 1, hops)), DMA((2, 2, hops, 4)), DMA((2, 2, hops, 4)), DMA((2, 2, hops, 3)), DMA((2, 2, hops, 3))]

time: 1280 us -> 1270 us (level)
  Pallas kernels: 1270 us -> 1250 us
    pallas_call x2, Pallas kernels: 1270 us -> 1250 us  [call_block(): pl.pallas_call(functools.partial(block_kernel, b, step), out_shape=tuple(...]
where the time goes in v3:
time: 1270 us; the launch traced here: 1260 us
  Pallas kernels  1250 us (98%)
    pallas_call x2, Pallas kernels, call_block(): pl.pallas_call(functools.partial(block_kernel, b, step), out_shape=tuple(...  1250 us

profile of v3, /device:TPU:1, one launch (start us, length us, event | category | flops | bytes accessed | tf_op | source)
XLA Modules:
  0.0 1256.4 jit_solution(9987272821702334205)
XLA Ops:
  0.0 682.1 %block_0.1 = (bf16[16,16,5120]{2,1,0:T(8,128)(2,1)}, bf16[4,4,64,5120]{3,2,1,0:T(8,128)(2,1)}, bf16[4,4,256,1280]{3,2,1,0:T(8,128)(2,1)}, bf16[4,256,1280]{2,1,0...) custom-call(bf16[4,64,5120]{2,1,0:T(8,128)(2,1)} %bitcast.16, ...), custom_call_target="tpu_custom_call" | custom-call | tf_op jit(solution)/shard_map/block_0/pallas_call | solution.py:671
  682.1 0.1 reshape.139
  682.3 4.1 convolution_convert_fusion.1
  686.4 565.3 %block_1.1 = (bf16[16,16,5120]{2,1,0:T(8,128)(2,1)}, bf16[4,4,64,5120]{3,2,1,0:T(8,128)(2,1)}, bf16[4,4,256,1280]{3,2,1,0:T(8,128)(2,1)}, bf16[4,256,1280]{2,1,0...) custom-call(bf16[4,64,5120]{2,1,0:T(8,128)(2,1)} %bitcast.13, ...), custom_call_target="tpu_custom_call", output_to_operand_aliasing={{5}: (7, {})} | custom-call | tf_op jit(solution)/shard_map/block_1/pallas_call | solution.py:671
  1251.7 0.1 reshape.132
  1251.8 4.1 convolution_convert_fusion
  (2 shorter events, 0.0 us)

commit v4 on v3

--- a/solution.py
+++ b/solution.py
@@ -582,6 +582,13 @@
                     def _():
                         hop_copy(d, c, far - 1, slot_of(d, c, far)).wait_send()
 
+    def settled(c):
+        reduce_sent(c)
+        turn_own(c).wait()
+        for k in range(3):
+            turn(c, k).wait_send()
+            turn_arrive(c, k)
+
     outward = lambda d: z == (LINE - 2 if d == 0 else 1)
     inward = lambda d: jnp.logical_not(outward(d))
     inner = lambda d: jnp.logical_and(z > 0, z < LINE - 1)
@@ -604,13 +611,15 @@
     Q, A, B = later(queries), later(attend), later(feed)
     RS, RR, F = later(reduce_start), later(reduce_relay), later(reduce_finish)
     early_half = reduce_early if early else hook()
+    rest = lambda d: jnp.logical_not(first(d))
+    ahead = [XS(c, h0, first) for c in (c1, c2, c3)]
     VS, VR = later(w1.along.start), later(w1.along.relay)
     VP, VF, VD = later(w1.spread), later(w1.forward), later(w1.forward_diagonal)
 
     if b == 0:
         US, UR, UP, UF, UD = (later(f) for f in (w0.along.start, w0.along.relay, w0.spread, w0.forward, w0.forward_diagonal))
-        lead = [US(c0, h0), UR(c0, h1), UP(h0), UR(c0, h2), XS(c0, h0), VS(c0, h0, first), XR(c0, h1), VS(c0, h0, both(inner, inward))]
-        lead += [UP(h1), UF(h0), UP(h2), XR(c0, h2), XS(c1, h0), XR(c1, h1)]
+        lead = [US(c0, h0), UR(c0, h1), UP(h0), UR(c0, h2), XS(c0, h0), *ahead, VS(c0, h0, first), XR(c0, h1), VS(c0, h0, both(inner, inward))]
+        lead += [UP(h1), UF(h0), UP(h2), XR(c0, h2), XS(c1, h0, rest), XR(c1, h1)]
         after_a0, after_q1, after_a1 = [UD(h0), UF(h1), UF(h2)], [UD(h1)], [UD(h2), later(w0.arrive)(range(h3))]
         after_b0, after_b1, after_rr13 = [VP(h0, inner, "always")], [VF(h0, inner)], [VD(h0, inner)]
         in_b2, after_b2 = [VS(c0, h0, both(inner, outward)), VR(c0, h1, outward, False)], [VR(c0, h1, inward, False)]
@@ -619,31 +628,26 @@
         tail2 = [VF(h1, inner)]
         tail3 = [VD(h0, outer), VD(h1, inner), VF(h1, outer)]
         last = [VD(h1, outer), later(w1.arrive)(range(h2))] + [later(w1.along.settle)(d, c0, h2) for d in range(h2)]
-        last += [later(w0.along.finish)(h1), later(w0.finish)(range(h3)), later(w1.along.finish)(h1), later(w1.finish)(range(h2))]
+        last += [later(w1.along.finish)(h1), later(w1.finish)(range(h2))]
+        done = [later(w0.along.finish)(h1), later(w0.finish)(range(h3))]
     else:
-        lead = [VP(h2, wait="never"), XS(c0, h0), XR(c0, h1), XR(c0, h2), XS(c1, h0), XR(c1, h1)]
-        after_a0, after_q1, after_a1, last = [VF(h2)], [VD(h2)], [later(w1.arrive)((h2,))], [later(w1.finish)((h2,))]
+        lead = [VP(h2, wait="never"), XS(c0, h0), *ahead, XR(c0, h1), XR(c0, h2), XS(c1, h0, rest), XR(c1, h1)]
+        after_a0, after_q1, after_a1, last, done = [VF(h2)], [VD(h2)], [later(w1.arrive)((h2,))], [], [later(w1.finish)((h2,))]
         after_b0 = after_b1 = after_rr13 = in_b2 = after_b2 = tail0 = tail1 = tail2 = tail3 = []
-    schedule = lead + [Q(c0, middle=XR(c1, h2)), A(c0), OS(c0, h0)] + after_a0 + [OR(c0, h1), Q(c1, middle=OR(c0, h2)), XS(c2, h0)] + after_q1
-    schedule += [A(c1)] + after_a1
-    schedule += [B(c0, mid_out=XR(c2, h1), after_out=XR(c2, h2), after_up=hook(OS(c1, h0), XS(c3, h0)), mid_down=early_half), RS(c0, outwards), OR(c1, h1)]
-    schedule += after_b0 + [Q(c2, middle=hook(OR(c1, h2), XR(c3, h1))), A(c2)]
-    schedule += [B(c1, mid_out=RR(c0, h3), after_out=XR(c3, h2), after_up=hook(OS(c2, h0), RR(c0, h2))), RS(c1, outwards[:1])] + after_b1
-    schedule += [Q(c3, middle=hook(OR(c2, h1), F(c0))), OR(c2, h2), A(c3), OS(c3, h0), RS(c1, outwards[1:]), RR(c1, h3)] + after_rr13
+    schedule = lead + [Q(c0, middle=XR(c1, h2)), A(c0), OS(c0, h0)] + after_a0 + [OR(c0, h1), Q(c1, middle=OR(c0, h2)), XS(c2, h0, rest)] + after_q1
+    schedule += [A(c1), OS(c1, h0, first)] + after_a1
+    schedule += [B(c0, mid_out=XR(c2, h1), after_out=XR(c2, h2), after_up=hook(OS(c1, h0, rest), XS(c3, h0, rest)), mid_down=early_half), RS(c0, outwards), OR(c1, h1)]
+    schedule += after_b0 + [Q(c2, middle=hook(OR(c1, h2), XR(c3, h1))), A(c2), OS(c2, h0, first)]
+    schedule += [B(c1, mid_out=RR(c0, h3), after_out=XR(c3, h2), after_up=hook(OS(c2, h0, rest), RR(c0, h2))), RS(c1, outwards[:h2])] + after_b1
+    schedule += [Q(c3, middle=hook(OR(c2, h1), F(c0))), OR(c2, h2), A(c3), OS(c3, h0), RS(c1, outwards[h2:]), RR(c1, h3)] + after_rr13
     schedule += [B(c2, mid_out=OR(c3, h1), after_out=OR(c3, h2), after_up=hook(RR(c1, h2), *in_b2)), RS(c2, outwards)] + after_b2
-    schedule += [B(c3, after_out=F(c1), after_up=RR(c2, h3)), RS(c3, outwards)] + tail0 + [RR(c2, h2)] + tail1 + [F(c2)] + tail2
-    schedule += [RR(c3, h3)] + tail3 + [RR(c3, h2), F(c3)] + last
+    schedule += [B(c3, mid_out=RR(c2, h3), after_up=RR(c2, h2)), RS(c3, outwards), F(c1)] + tail0 + tail1 + [RR(c3, h3), F(c2)] + tail2
+    done += [later(xg.finish)(chunks), later(og_.finish)(chunks)] + [later(settled)(c) for c in range(c3)]
+    schedule += tail3 + [RR(c3, h2)] + done + [F(c3)] + last
     meet(line, (CORE, Y, X, Y_CORE))
     for action in schedule:
         action()
-    xg.finish(chunks)
-    og_.finish(chunks)
-    for c in range(chunks):
-        reduce_sent(c)
-        turn_own(c).wait()
-        for k in range(3):
-            turn(c, k).wait_send()
-            turn_arrive(c, k)
+    settled(c3)
 
 
 ANY = pl.BlockSpec(memory_space=pl.ANY)

time: 1270 us -> 1250 us (0.984)
  Pallas kernels: 1250 us -> 1230 us
    pallas_call x2, Pallas kernels: 1250 us -> 1230 us  [call_block(): pl.pallas_call(functools.partial(block_kernel, b, step), out_shape=tuple(...]
where the time goes in v4:
time: 1250 us; the launch traced here: 1240 us
  Pallas kernels  1230 us (98%)
    pallas_call x2, Pallas kernels, call_block(): pl.pallas_call(functools.partial(block_kernel, b, step), out_shape=tuple(...  1230 us

profile of v4, /device:TPU:1, one launch (start us, length us, event | category | flops | bytes accessed | tf_op | source)
XLA Modules:
  0.0 1235.9 jit_solution(5503954597913674038)
XLA Ops:
  0.0 682.3 %block_0.1 = (bf16[16,16,5120]{2,1,0:T(8,128)(2,1)}, bf16[4,4,64,5120]{3,2,1,0:T(8,128)(2,1)}, bf16[4,4,256,1280]{3,2,1,0:T(8,128)(2,1)}, bf16[4,256,1280]{2,1,0...) custom-call(bf16[4,64,5120]{2,1,0:T(8,128)(2,1)} %bitcast.16, ...), custom_call_target="tpu_custom_call" | custom-call | tf_op jit(solution)/shard_map/block_0/pallas_call | solution.py:675
  682.3 0.1 reshape.139
  682.4 4.1 convolution_convert_fusion.1
  686.6 544.7 %block_1.1 = (bf16[16,16,5120]{2,1,0:T(8,128)(2,1)}, bf16[4,4,64,5120]{3,2,1,0:T(8,128)(2,1)}, bf16[4,4,256,1280]{3,2,1,0:T(8,128)(2,1)}, bf16[4,256,1280]{2,1,0...) custom-call(bf16[4,64,5120]{2,1,0:T(8,128)(2,1)} %bitcast.13, ...), custom_call_target="tpu_custom_call", output_to_operand_aliasing={{5}: (7, {})} | custom-call | tf_op jit(solution)/shard_map/block_1/pallas_call | solution.py:675
  1231.3 0.1 reshape.132
  1231.4 4.1 convolution_convert_fusion
  (2 shorter events, 0.0 us)
